TPU v7x, 128 devices: a whole 4x4x4 slice. The times are simulated.
128 devices in a mesh: col: 2 (over core), row: 64 (over z, y, x).
Axes of the slice: x: 4, y: 4, z: 4, core: 2. Of those that a mesh axis runs over, the one named last changes fastest.
Arguments:
- hyper_params: float32 [3], replicated
- w_in: float32 [16, 1024, 2816], P(None, 'row', 'col')
- x_in: bfloat16 [16, 1024, 1024], P(None, None, 'row')
- dy_in: bfloat16 [16, 1024, 2816], P(None, None, 'col')
- row_in: float32 [16, 1024], P(None, 'row')
- col_in: float32 [16, 2816], P(None, 'col')
- w_out: float32 [16, 2816, 1024], P(None, 'col', 'row')
- x_out: bfloat16 [16, 1024, 2816], P(None, None, 'col')
- dy_out: bfloat16 [16, 1024, 1024], P(None, None, 'row')
- row_out: float32 [16, 2816], P(None, 'col')
- col_out: float32 [16, 1024], P(None, 'row')
Outputs:
- output 1: float32 [16, 1024, 2816], P(None, 'row', 'col')
- output 2: float32 [16, 1024], P(None, 'row')
- output 3: float32 [16, 2816], P(None, 'col')
- output 4: float32 [16, 2816, 1024], P(None, 'col', 'row')
- output 5: float32 [16, 2816], P(None, 'col')
- output 6: float32 [16, 1024], P(None, 'row')
All inputs are finite; a program needn't handle non-finite values.
Results may differ from a plain program's by a relative error of at most 0.001.
Values are sent between devices in bfloat16 or wider.
A program may use at most 1 GiB of HBM per device.

v0:
```python
import jax
import jax.numpy as jnp
from jax import lax
from jax.sharding import PartitionSpec as P

EPS_ONE = 1e-30
EPS_TWO = 1e-3
BOTH_AXES = ('col', 'row')


def update_block(w_blk, x_blk, dy_blk, row_old, col_old, hyper_params, rows_axis, cols_axis, n_rows, n_cols):
    beta_two = hyper_params[0]
    rho_step = hyper_params[1]
    clip_max = hyper_params[2]
    n_total = float(n_rows * n_cols)
    grad_blk = lax.dot_general(x_blk, dy_blk, (((0,), (0,)), ((), ())), preferred_element_type=jnp.float32)
    sq_grad = grad_blk * grad_blk + EPS_ONE
    row_part = jnp.sum(sq_grad, axis=1)
    col_part = jnp.sum(sq_grad, axis=0)
    lead_col = (lax.axis_index(cols_axis) == 0).astype(jnp.float32)
    scalars = jnp.stack([jnp.sum(row_part), jnp.sum(w_blk * w_blk), lead_col * jnp.sum(row_old)])
    row_sum = lax.psum(row_part, cols_axis)
    col_sum = lax.psum(col_part, rows_axis)
    scalar_sum = lax.psum(scalars, BOTH_AXES)
    row_new = beta_two * row_old + (1.0 - beta_two) * (row_sum / n_cols)
    col_new = beta_two * col_old + (1.0 - beta_two) * (col_sum / n_rows)
    row_mean = beta_two * (scalar_sum[2] / n_rows) + (1.0 - beta_two) * (scalar_sum[0] / n_total)
    update = grad_blk * lax.rsqrt((row_new / row_mean)[:, None] * col_new[None, :])
    upd_sq = lax.psum(jnp.sum(update * update), BOTH_AXES)
    upd_rms = jnp.sqrt(upd_sq / n_total)
    w_rms = jnp.sqrt(scalar_sum[1] / n_total)
    step_size = rho_step * jnp.maximum(EPS_TWO, w_rms) / jnp.maximum(1.0, upd_rms / clip_max)
    return w_blk - step_size * update, row_new, col_new


def solution(mesh):
    n_col = mesh.shape['col']
    n_row = mesh.shape['row']
    tile_in = P(None, 'row', 'col')
    tile_out = P(None, 'col', 'row')
    lane_row = P(None, None, 'row')
    lane_col = P(None, None, 'col')
    vec_row = P(None, 'row')
    vec_col = P(None, 'col')

    def local_step(hyper_params, w_in, x_in, dy_in, row_in, col_in, w_out, x_out, dy_out, row_out, col_out):
        d_model = w_in.shape[1] * n_row
        d_hidden = w_in.shape[2] * n_col
        results = []
        for layer_idx in range(w_in.shape[0]):
            in_result = update_block(w_in[layer_idx], x_in[layer_idx], dy_in[layer_idx], row_in[layer_idx], col_in[layer_idx], hyper_params, 'row', 'col', d_model, d_hidden)
            out_result = update_block(w_out[layer_idx], x_out[layer_idx], dy_out[layer_idx], row_out[layer_idx], col_out[layer_idx], hyper_params, 'col', 'row', d_hidden, d_model)
            results.append(in_result + out_result)
        return tuple(jnp.stack([res_item[out_idx] for res_item in results]) for out_idx in range(6))

    return jax.shard_map(local_step, mesh=mesh, in_specs=(P(), tile_in, lane_row, lane_col, vec_row, vec_col, tile_out, lane_col, lane_row, vec_col, vec_row), out_specs=(tile_in, vec_row, vec_col, tile_out, vec_col, vec_row), check_vma=False)
```

profile of v0, /device:TPU:1, one launch (start us, length us, event | category | flops | bytes accessed | tf_op | source)
XLA Modules:
  0.0 662.3 jit_solution(3693308601625090600)
XLA Ops:
  7.2 3.7 fusion.192
  10.9 3.6 fusion.189
  14.6 3.6 fusion.186
  18.2 3.6 fusion.183
  21.9 3.6 fusion.180
  25.5 3.7 fusion.177
  50.4 3.6 fusion.153
  54.1 3.7 fusion.150
  57.7 3.7 fusion.147
  61.4 3.7 fusion.144
  65.0 3.6 fusion.141
  68.7 3.6 fusion.138
  72.3 3.7 fusion.135
  76.0 3.7 fusion.132
  79.7 3.7 fusion.129
  86.9 3.6 fusion.219
  94.2 3.7 fusion.213
  97.8 3.6 fusion.210
  101.4 3.6 fusion.207
  105.1 3.6 fusion.204
  115.9 3.7 fusion.195
  208.9 70.4 %all-reduce.1 = (f32[3]{0:T(128)}, f32[3]{0:T(128)}, f32[3]{0:T(128)}, f32[3]{0:T(128)}, f32[3]{0:T(128)}, /*index=5*/f32[3]{0:T(128)}, f32[3]{0:T(128)}, f32[3]...) all-reduce(f32[3]{0:T(128)} %pad_maximum_fusion, ...), channel_id=1, replica_groups=mesh['col'=2,'row'=64] {'col','row'}, use_global_device_ids=true, to_apply=%region_3.0 | all-reduce | flops 96 | bytes 768 | tf_op jit(solution)/shard_map/psum | solution.py:24
  339.4 5.8 all-reduce.3
  496.8 64.2 %all-reduce = (f32[]{:T(128)}, f32[]{:T(128)}, f32[]{:T(128)}, f32[]{:T(128)}, f32[]{:T(128)}, /*index=5*/f32[]{:T(128)}, f32[]{:T(128)}, f32[]{:T(128)}, f32[]{...) all-reduce(f32[]{:T(128)} %multiply_reduce_fusion.31, ...), channel_id=1, replica_groups=mesh['col'=2,'row'=64] {'col','row'}, use_global_device_ids=true, to_apply=%region_9.0 | all-reduce | flops 32 | bytes 256 | tf_op jit(solution)/shard_map/psum | solution.py:29
  (475 shorter events, 261.7 us)
Async XLA Ops:
  7.2 433.9 %all-reduce.6.cloned.1.call-start = ((), (), s32[]{:S(2)}) async-start(), calls=%async_computation | async-start | bytes 524288 | tf_op jit(solution)/shard_map/psum | solution.py:23
  348.7 86.6 %copy-start.96 = (f32[16]{0:T(128)}, f32[16]{0:T(128)S(1)}, u32[]{:S(2)}) copy-start(f32[16]{0:T(128)S(1)} %get-tuple-element.390) | copy-start | bytes 196
  348.7 86.6 %copy-start.98 = (f32[16]{0:T(128)}, f32[16]{0:T(128)S(1)}, u32[]{:S(2)}) copy-start(f32[16]{0:T(128)S(1)} %get-tuple-element.391) | copy-start | bytes 196
  348.7 86.6 %copy-start.100 = (f32[16]{0:T(128)}, f32[16]{0:T(128)S(1)}, u32[]{:S(2)}) copy-start(f32[16]{0:T(128)S(1)} %get-tuple-element.392) | copy-start | bytes 196
  351.0 84.4 %copy-start.102 = (f32[16]{0:T(128)}, f32[16]{0:T(128)S(1)}, u32[]{:S(2)}) copy-start(f32[16]{0:T(128)S(1)} %get-tuple-element.398) | copy-start | bytes 196
  441.3 37.2 %copy-start.27 = (f32[1408,16]{0,1:T(8,128)S(1)}, f32[1408,16]{0,1:T(8,128)}, u32[]{:S(2)}) copy-start(f32[1408,16]{0,1:T(8,128)} %get-tuple-element.551) | copy-start | bytes 270340
  441.3 37.2 %copy-start.109 = (f32[16]{0:T(128)S(1)}, f32[16]{0:T(128)}, u32[]{:S(2)}) copy-start(f32[16]{0:T(128)} %get-tuple-element.399) | copy-start | bytes 196
  441.3 37.9 %copy-start.13 = (f32[1408,16]{0,1:T(8,128)S(1)}, f32[1408,16]{0,1:T(8,128)}, u32[]{:S(2)}) copy-start(f32[1408,16]{0,1:T(8,128)} %get-tuple-element.550) | copy-start | bytes 270340
  441.3 37.9 %copy-start.110 = (f32[16]{0:T(128)S(1)}, f32[16]{0:T(128)}, u32[]{:S(2)}) copy-start(f32[16]{0:T(128)} %get-tuple-element.400) | copy-start | bytes 196
  441.3 38.6 %copy-start.14 = (f32[1408,16]{0,1:T(8,128)S(1)}, f32[1408,16]{0,1:T(8,128)}, u32[]{:S(2)}) copy-start(f32[1408,16]{0,1:T(8,128)} %get-tuple-element.549) | copy-start | bytes 270340
  441.4 38.6 %copy-start.111 = (f32[16]{0:T(128)S(1)}, f32[16]{0:T(128)}, u32[]{:S(2)}) copy-start(f32[16]{0:T(128)} %get-tuple-element.401) | copy-start | bytes 196
  441.4 39.4 %copy-start.16 = (f32[1408,16]{0,1:T(8,128)S(1)}, f32[1408,16]{0,1:T(8,128)}, u32[]{:S(2)}) copy-start(f32[1408,16]{0,1:T(8,128)} %get-tuple-element.548) | copy-start | bytes 270340
  441.4 39.4 %copy-start.112 = (f32[16]{0:T(128)S(1)}, f32[16]{0:T(128)}, u32[]{:S(2)}) copy-start(f32[16]{0:T(128)} %get-tuple-element.402) | copy-start | bytes 196
  441.4 40.2 %copy-start.18 = (f32[1408,16]{0,1:T(8,128)S(1)}, f32[1408,16]{0,1:T(8,128)}, u32[]{:S(2)}) copy-start(f32[1408,16]{0,1:T(8,128)} %get-tuple-element.547) | copy-start | bytes 270340
  442.4 40.5 %copy-start.45 = (f32[1408]{0:T(1024)}, f32[1408]{0:T(1024)S(1)}, u32[]{:S(2)}) copy-start(f32[1408]{0:T(1024)S(1)} %get-tuple-element.326) | copy-start | bytes 16900
  442.4 40.5 %copy-start.46 = (f32[1408]{0:T(1024)}, f32[1408]{0:T(1024)S(1)}, u32[]{:S(2)}) copy-start(f32[1408]{0:T(1024)S(1)} %get-tuple-element.561) | copy-start | bytes 16900
  443.6 39.3 %copy-start.20 = (f32[1408,16]{0,1:T(8,128)S(1)}, f32[1408,16]{0,1:T(8,128)}, u32[]{:S(2)}) copy-start(f32[1408,16]{0,1:T(8,128)} %get-tuple-element.546) | copy-start | bytes 270340
  444.4 39.2 %copy-start.47 = (f32[1408]{0:T(1024)}, f32[1408]{0:T(1024)S(1)}, u32[]{:S(2)}) copy-start(f32[1408]{0:T(1024)S(1)} %get-tuple-element.330) | copy-start | bytes 16900
  444.4 39.2 %copy-start.48 = (f32[1408]{0:T(1024)}, f32[1408]{0:T(1024)S(1)}, u32[]{:S(2)}) copy-start(f32[1408]{0:T(1024)S(1)} %get-tuple-element.563) | copy-start | bytes 16900
  445.6 38.0 %copy-start.29 = (f32[1408,16]{0,1:T(8,128)S(1)}, f32[1408,16]{0,1:T(8,128)}, u32[]{:S(2)}) copy-start(f32[1408,16]{0,1:T(8,128)} %get-tuple-element.545) | copy-start | bytes 270340
  446.4 38.0 %copy-start.49 = (f32[1408]{0:T(1024)}, f32[1408]{0:T(1024)S(1)}, u32[]{:S(2)}) copy-start(f32[1408]{0:T(1024)S(1)} %get-tuple-element.334) | copy-start | bytes 16900
  446.4 38.0 %copy-start.50 = (f32[1408]{0:T(1024)}, f32[1408]{0:T(1024)S(1)}, u32[]{:S(2)}) copy-start(f32[1408]{0:T(1024)S(1)} %get-tuple-element.565) | copy-start | bytes 16900
  448.4 36.8 %copy-start.51 = (f32[1408]{0:T(1024)}, f32[1408]{0:T(1024)S(1)}, u32[]{:S(2)}) copy-start(f32[1408]{0:T(1024)S(1)} %get-tuple-element.338) | copy-start | bytes 16900
  448.4 36.8 %copy-start.52 = (f32[1408]{0:T(1024)}, f32[1408]{0:T(1024)S(1)}, u32[]{:S(2)}) copy-start(f32[1408]{0:T(1024)S(1)} %get-tuple-element.567) | copy-start | bytes 16900
  (115 other events, 2351.9 us)
Sparse Core Ops, SparseCore 0:
  119.8 157.7 all-reduce.5
where the time goes:
time: 669 us; the launch traced here: 662 us
  between operations  183 us (27%)
  other arithmetic  167 us (25%)
  blocking collectives  140 us (21%)
  matrix products  112 us (17%)
  local copies, waits for them, and re-layouts  58.8 us (9%)
    dot_general x32, matrix products, update_block(): lax.dot_general(x_blk, dy_blk, (((0,), (0,)), ((), ())), preferred_elemen...  112 us
    psum x1, blocking collectives, update_block(): scalar_sum = lax.psum(scalars, BOTH_AXES)  70.4 us
    psum x1, blocking collectives, update_block(): upd_sq = lax.psum(jnp.sum(update * update), BOTH_AXES)  64.2 us
    another operation x32, other arithmetic, update_block(): jnp.stack([jnp.sum(row_part), jnp.sum(w_blk * w_blk), lead_col * jnp.sum(...  60.1 us
    unnamed x30, other arithmetic  46.3 us
    slice x24, local copies, waits for them, and re-layouts, update_block(): w_rms = jnp.sqrt(scalar_sum[1] / n_total)  30.7 us
    reduce_sum x32, other arithmetic, update_block(): upd_sq = lax.psum(jnp.sum(update * update), BOTH_AXES)  24.2 us
    another operation x20, local copies, waits for them, and re-layouts, local_step(): jnp.stack([res_item[out_idx] for res_item in results])  17.4 us
  transfers between devices with their start and end apart: 1, of which 0 were waited for; matrix products, arithmetic and copies ran while one was open for 18% of the time, Pallas kernels for 0%

commit v1 on v0

v1 whole, which is shorter than its diff:
```python
import functools

import jax
import jax.numpy as jnp
from jax import lax
from jax.experimental import pallas as pl
from jax.experimental.pallas import tpu as pltpu
from jax.sharding import PartitionSpec as P

EPS_ONE = 1e-30
EPS_TWO = 1e-3
MESH = pl.DeviceIdType.MESH
LANES = 128
SLOTS = 10
LAG = 2


def torus_dims(n_row):
    side = round(n_row ** (1.0 / 3.0))
    return side, side, side


def kernel(dims, hyper, a_in, b_in, w_in, side_in, lane_in, a_out, b_out, w_out, lane_out, side_out,
           o_w_in, o_side_in, o_lane_in, o_w_out, o_lane_out, o_side_out,
           hyper_s, a_v, b_v, g_v, w_v, side_old, lane_old, side_res, lane_res, old_pack, side_new,
           fac_v, new_pack, row_buf, aux_buf, x_buf, y_buf, z_buf, acc_v, fx_buf, fy_buf, fz_buf,
           load_sem, b_sem, store_sem, send_sem, x_sem, aux_sem, row_sem, y_sem, z_sem, f_sem):
    nz, ny, nx = dims
    layers, _, width = w_in.shape
    depth = a_in.shape[1]
    chunks = width // LANES
    n_row = nz * ny * nx
    n_side = float(depth * n_row)
    n_lane = float(width * 2)
    n_total = n_side * n_lane

    row = lax.axis_index("row")
    core = lax.axis_index("col")
    my_x = lax.rem(row, nx)
    my_y = lax.rem(row // nx, ny)
    my_z = row // (nx * ny)

    def dev(z, y, x, c):
        return {"row": (z * ny + y) * nx + x, "col": c}

    other = 1 - core
    x_peers = [lax.rem(my_x + d, nx) for d in range(1, nx)]
    y_peers = [lax.rem(my_y + d, ny) for d in range(1, ny)]
    z_peers = [lax.rem(my_z + d, nz) for d in range(1, nz)]
    x_devs = [dev(my_z, my_y, x, core) for x in x_peers]
    c_devs = [dev(my_z, my_y, x, other) for x in x_peers + [my_x]]
    y_devs = [dev(my_z, y, my_x, core) for y in y_peers]
    z_devs = [dev(z, my_y, my_x, core) for z in z_peers]
    partner = c_devs[-1]

    b_refs = (b_in, b_out)

    def b_copy(layer, j):
        slot = lax.rem(2 * layer + j, SLOTS)
        return pltpu.make_async_copy(b_refs[j].at[layer], b_v.at[slot], b_sem.at[slot])

    small = [(hyper, hyper_s), (a_in, a_v.at[0]), (a_out, a_v.at[1]), (side_in, side_old.at[0]), (side_out, side_old.at[1]),
             (lane_in, lane_old.at[0]), (lane_out, lane_old.at[1])]
    small = [pltpu.make_async_copy(s, d, load_sem.at[i]) for i, (s, d) in enumerate(small)]
    big = [pltpu.make_async_copy(s, w_v.at[j], load_sem.at[len(small) + j]) for j, s in enumerate((w_in, w_out))]
    for c in small:
        c.start()
    for s in range(SLOTS):
        b_copy(s // 2, s % 2).start()
        if s == 3:
            for c in big:
                c.start()

    barrier = pltpu.get_barrier_semaphore()
    peers = x_devs + c_devs + y_devs + z_devs
    for d in peers:
        pl.semaphore_signal(barrier, inc=1, device_id=d, device_id_type=MESH)
    for c in small:
        c.wait()
    acc_v[...] = jnp.zeros_like(acc_v)
    beta = hyper_s[0]
    keep = 1.0 - beta
    eye = lax.broadcasted_iota(jnp.int32, (depth, depth), 0) == lax.broadcasted_iota(jnp.int32, (depth, depth), 1)
    lane_id = lax.broadcasted_iota(jnp.int32, (1, LANES), 1)
    pack_rows = x_buf.shape[2]
    pack_id = lax.broadcasted_iota(jnp.int32, (pack_rows, LANES), 0)
    aux_row = pack_rows - 8

    for layer in range(layers):
        for j in range(2):
            for k in range(chunks):
                old_pack[layer, j * chunks + k:j * chunks + k + 1, :] = lane_old[j, layer:layer + 1, k * LANES:(k + 1) * LANES]
            line = jnp.broadcast_to(side_old[j, layer:layer + 1, :], (depth, depth))
            line = jnp.sum(jnp.where(eye, line, 0.0), axis=1, keepdims=True)
            side_new[layer, j * depth:(j + 1) * depth, :] = jnp.broadcast_to(line, (depth, LANES))
        old_pack[layer, 2 * chunks:, :] = jnp.ones((pack_rows - 2 * chunks, LANES), jnp.float32)
    pl.semaphore_wait(barrier, len(peers))

    def send(src, dst, recv, d, k):
        pltpu.make_async_remote_copy(src_ref=src, dst_ref=dst, send_sem=send_sem.at[k], recv_sem=recv, device_id=d, device_id_type=MESH).start()

    def arrived(ref, sem):
        pltpu.make_async_copy(ref, ref, sem).wait()

    def stage_a(layer):
        for j in range(2):
            b_copy(layer, j).wait()
            slot = lax.rem(2 * layer + j, SLOTS)
            grad = jnp.dot(a_v[j, layer], b_v[slot], preferred_element_type=jnp.float32)
            nxt = layer + SLOTS // 2

            @pl.when(nxt < layers)
            def _():
                b_copy(nxt, j).start()

            g_v[j, layer] = grad
            sq = grad * grad + EPS_ONE
            lane_part = jnp.sum(sq, axis=0, keepdims=True)
            side_part = sq[:, :LANES]
            total = lane_part[:, :LANES]
            for k in range(chunks):
                cols = slice(k * LANES, (k + 1) * LANES)
                if k:
                    side_part = side_part + sq[:, cols]
                    total = total + lane_part[:, cols]
                x_buf[layer, my_x, j * chunks + k:j * chunks + k + 1, :] = lane_part[:, cols]
            row_buf[layer, core, j * depth:(j + 1) * depth, :] = side_part
            mean_part = total * (keep / n_total)
            if j == 0:
                old = jnp.sum(side_new[layer, :depth, :], axis=0, keepdims=True)
                mean_part = mean_part + old * (0.5 * beta / (n_side * LANES))
            else:
                old = jnp.sum(jnp.where((pack_id >= chunks) & (pack_id < 2 * chunks), old_pack[layer], 0.0), axis=0, keepdims=True)
                mean_part = mean_part + old * (beta / (n_lane * n_row))
            x_buf[layer, my_x, 2 * chunks + j:2 * chunks + j + 1, :] = mean_part
        for d in x_devs:
            send(x_buf.at[layer, my_x], x_buf.at[layer, my_x], x_sem.at[layer], d, 0)
        send(row_buf.at[layer, core], row_buf.at[layer, core], row_sem.at[layer], partner, 1)
        for d in c_devs:
            send(x_buf.at[layer, my_x, pl.ds(aux_row, 8)], aux_buf.at[layer, my_x], aux_sem.at[layer], d, 2)

    def stage_x(layer):
        arrived(x_buf.at[layer, pl.ds(0, nx - 1)], x_sem.at[layer])
        arrived(aux_buf.at[layer], aux_sem.at[layer])
        tot = x_buf[layer, 0]
        aux = aux_buf[layer, 0]
        for s in range(1, nx):
            tot = tot + x_buf[layer, s]
            aux = aux + aux_buf[layer, s]
        y_buf[layer, my_y] = tot
        tail = tot[aux_row:, :]
        last = lax.broadcasted_iota(jnp.int32, (8, LANES), 0) >= 2 * chunks - aux_row
        y_buf[layer, my_y, aux_row:, :] = jnp.where(last, tail + aux, tail)
        for d in y_devs:
            send(y_buf.at[layer, my_y], y_buf.at[layer, my_y], y_sem.at[layer], d, 3)
        arrived(row_buf.at[layer, 0], row_sem.at[layer])
        side_sum = jnp.sum(row_buf[layer, 0] + row_buf[layer, 1], axis=1, keepdims=True)
        side_new[layer] = beta * side_new[layer] + side_sum * (keep / n_lane)

    def stage_y(layer):
        arrived(y_buf.at[layer, pl.ds(0, ny - 1)], y_sem.at[layer])
        tot = y_buf[layer, 0]
        for s in range(1, ny):
            tot = tot + y_buf[layer, s]
        z_buf[layer, my_z] = tot
        for d in z_devs:
            send(z_buf.at[layer, my_z], z_buf.at[layer, my_z], z_sem.at[layer], d, 4)

    def stage_z(layer):
        arrived(z_buf.at[layer, pl.ds(0, nz - 1)], z_sem.at[layer])
        tot = z_buf[layer, 0]
        for s in range(1, nz):
            tot = tot + z_buf[layer, s]
        new = beta * old_pack[layer] + tot * (keep / n_side)
        new_pack[layer] = new
        mean = [jnp.sum(tot[2 * chunks + j:2 * chunks + j + 1, :], axis=1, keepdims=True) for j in range(2)]
        fac_v[...] = lax.rsqrt(jnp.where(pack_id < chunks, new, new / mean[1]))
        for j in range(2):
            side = side_new[layer, j * depth:(j + 1) * depth, :]
            side = lax.rsqrt(side / mean[0] if j == 0 else side)
            u_sq = None
            w_sq = None
            for k in range(chunks):
                cols = slice(k * LANES, (k + 1) * LANES)
                line = slice(j * chunks + k, j * chunks + k + 1)
                upd = g_v[j, layer, :, cols] * side * fac_v[line, :]
                g_v[j, layer, :, cols] = upd
                wgt = w_v[j, layer, :, cols]
                u_sq = upd * upd if k == 0 else u_sq + upd * upd
                w_sq = wgt * wgt if k == 0 else w_sq + wgt * wgt
            for i, part in enumerate((u_sq, w_sq)):
                part = jnp.sum(jnp.sum(part, axis=0, keepdims=True), axis=1, keepdims=True)
                line = slice(2 * i + j, 2 * i + j + 1)
                acc_v[line, :] = acc_v[line, :] + jnp.where(lane_id == layer, part, 0.0)

    def step(i, carry):
        pl.when(i < layers)(lambda: stage_a(i))
        pl.when((i >= LAG) & (i < layers + LAG))(lambda: stage_x(i - LAG))
        pl.when((i >= 2 * LAG) & (i < layers + 2 * LAG))(lambda: stage_y(i - 2 * LAG))

        @pl.when(i == 3 * LAG)
        def _():
            for c in big:
                c.wait()

        pl.when(i >= 3 * LAG)(lambda: stage_z(i - 3 * LAG))
        return carry

    lax.fori_loop(0, layers + 3 * LAG, step, 0)

    stores = [(side_res.at[0], o_side_in), (side_res.at[1], o_side_out), (lane_res.at[0], o_lane_in), (lane_res.at[1], o_lane_out)]
    stores = [pltpu.make_async_copy(s, d, store_sem.at[i]) for i, (s, d) in enumerate(stores)]

    def total(buf):
        out = buf[0]
        for s in range(1, buf.shape[0]):
            out = out + buf[s]
        return out

    slot = core * nx + my_x
    fx_buf[slot] = acc_v[...]
    for d in x_devs + c_devs:
        send(fx_buf.at[slot], fx_buf.at[slot], f_sem.at[0], d, 5)
    for layer in range(layers):
        for j in range(2):
            for k in range(chunks):
                lane_res[j, layer:layer + 1, k * LANES:(k + 1) * LANES] = new_pack[layer, j * chunks + k:j * chunks + k + 1, :]
            line = side_new[layer, j * depth:(j + 1) * depth, :depth]
            side_res[j, layer:layer + 1, :] = jnp.sum(jnp.where(eye, line, 0.0), axis=0, keepdims=True)
    for c in stores:
        c.start()
    arrived(fx_buf.at[pl.ds(0, 2 * nx - 1)], f_sem.at[0])
    fy_buf[my_y] = total(fx_buf)
    for d in y_devs:
        send(fy_buf.at[my_y], fy_buf.at[my_y], f_sem.at[1], d, 6)
    arrived(fy_buf.at[pl.ds(0, ny - 1)], f_sem.at[1])
    fz_buf[my_z] = total(fy_buf)
    for d in z_devs:
        send(fz_buf.at[my_z], fz_buf.at[my_z], f_sem.at[2], d, 7)
    arrived(fz_buf.at[pl.ds(0, nz - 1)], f_sem.at[2])
    tot = total(fz_buf)
    rms = jnp.sqrt(tot / n_total)
    rho = hyper_s[1]
    clip = hyper_s[2]
    scale = rho * jnp.maximum(EPS_TWO, rms[2:4, :]) / jnp.maximum(1.0, rms[0:2, :] / clip)
    o_w = (o_w_in, o_w_out)

    def finish(layer, carry):
        for j in range(2):
            amount = jnp.sum(jnp.where(lane_id == layer, scale[j:j + 1, :], 0.0), axis=1, keepdims=True)
            w_v[j, layer] = w_v[j, layer] - amount * g_v[j, layer]
            pltpu.make_async_copy(w_v.at[j, layer], o_w[j].at[layer], store_sem.at[4 + j]).start()
        return carry

    lax.fori_loop(0, layers, finish, 0)

    def sent(ref, k):
        pltpu.make_async_copy(ref, ref, send_sem.at[k]).wait()

    sent(x_buf.at[:, pl.ds(0, nx - 1)], 0)
    sent(row_buf.at[:, 0], 1)
    sent(aux_buf, 2)
    sent(y_buf.at[:, pl.ds(0, ny - 1)], 3)
    sent(z_buf.at[:, pl.ds(0, nz - 1)], 4)
    sent(fx_buf.at[pl.ds(0, 2 * nx - 1)], 5)
    sent(fy_buf.at[pl.ds(0, ny - 1)], 6)
    sent(fz_buf.at[pl.ds(0, nz - 1)], 7)
    for c in stores:
        c.wait()
    for j in range(2):
        pltpu.make_async_copy(w_v.at[j], o_w[j], store_sem.at[4 + j]).wait()


def solution(mesh):
    dims = torus_dims(mesh.shape['row'])
    nz, ny, nx = dims
    tile_in = P(None, 'row', 'col')
    tile_out = P(None, 'col', 'row')
    lane_row = P(None, None, 'row')
    lane_col = P(None, None, 'col')
    vec_row = P(None, 'row')
    vec_col = P(None, 'col')

    def local_step(hyper_params, w_in, x_in, dy_in, row_in, col_in, w_out, x_out, dy_out, row_out, col_out):
        layers, depth, width = w_in.shape
        tokens = x_in.shape[1]
        chunks = width // LANES
        pack = -(-(2 * chunks + 2) // 8) * 8
        f32 = jnp.float32
        turn = lambda v: jnp.swapaxes(v, 1, 2)
        vm = pltpu.VMEM
        dma = pltpu.SemaphoreType.DMA
        scratch = [
            pltpu.SMEM((3,), f32), vm((2, layers, depth, tokens), jnp.bfloat16), vm((SLOTS, tokens, width), jnp.bfloat16),
            vm((2, layers, depth, width), f32), vm((2, layers, depth, width), f32),
            vm((2, layers, depth), f32), vm((2, layers, width), f32), vm((2, layers, depth), f32), vm((2, layers, width), f32),
            vm((layers, pack, LANES), f32), vm((layers, 2 * depth, LANES), f32), vm((pack, LANES), f32), vm((layers, pack, LANES), f32),
            vm((layers, 2, 2 * depth, LANES), f32), vm((layers, nx, 8, LANES), f32),
            vm((layers, nx, pack, LANES), f32), vm((layers, ny, pack, LANES), f32), vm((layers, nz, pack, LANES), f32),
            vm((8, LANES), f32), vm((2 * nx, 8, LANES), f32), vm((ny, 8, LANES), f32), vm((nz, 8, LANES), f32),
            dma((9,)), dma((SLOTS,)), dma((6,)), dma((8,)), dma((layers,)), dma((layers,)), dma((layers,)), dma((layers,)), dma((layers,)), dma((3,)),
        ]
        shape = lambda *s: jax.ShapeDtypeStruct(s, f32)
        res = pl.pallas_call(
            functools.partial(kernel, dims),
            out_shape=(shape(layers, depth, width), shape(layers, depth), shape(layers, width), shape(layers, depth, width), shape(layers, width), shape(layers, depth)),
            in_specs=[pl.BlockSpec(memory_space=pl.ANY)] * 11,
            out_specs=[pl.BlockSpec(memory_space=pl.ANY)] * 6,
            scratch_shapes=scratch,
            name="adafactor_step",
            compiler_params=pltpu.CompilerParams(collective_id=0, has_side_effects=True, vmem_limit_bytes=60 * 1024 * 1024),
        )(hyper_params, turn(x_in), dy_in, w_in, row_in, col_in, turn(dy_out), x_out, turn(w_out), row_out, col_out)
        return res[0], res[1], res[2], turn(res[3]), res[4], res[5]

    return jax.shard_map(local_step, mesh=mesh, in_specs=(P(), tile_in, lane_row, lane_col, vec_row, vec_col, tile_out, lane_col, lane_row, vec_col, vec_row), out_specs=(tile_in, vec_row, vec_col, tile_out, vec_col, vec_row), check_vma=False)
```

time: 669 us -> 71 us (0.11)
  between operations: 183 us -> 0.67 us
  other arithmetic: 167 us -> 0 us
  blocking collectives: 140 us -> 0 us
  matrix products: 112 us -> 0 us
  Pallas kernels: 0 us -> 63.2 us
  local copies, waits for them, and re-layouts: 58.8 us -> 6.26 us
    psum x3 -> x0, blocking collectives: 140 us -> none  [the longest x1 70.4 us: update_block(): scalar_sum = lax.psum(scalars, BOTH_AXES)]
    dot_general x32 -> x0, matrix products: 112 us -> none  [update_block(): lax.dot_general(x_blk, dy_blk, (((0,), (0,)), ((), ())), preferred_elemen...]
    pallas_call x0 -> x1, Pallas kernels: none -> 63.2 us  [local_step(): pl.pallas_call(functools.partial(kernel, dims), out_shape=(shape(layers,...]
    another operation x34 -> x0, other arithmetic: 62.4 us -> none  [the longest x32 60.1 us: update_block(): jnp.stack([jnp.sum(row_part), jnp.sum(w_blk * w_blk), lead_col * jnp.sum(...]
    unnamed x30 -> x0, other arithmetic: 46.3 us -> none
    slice x25 -> x0, local copies, waits for them, and re-layouts: 31.3 us -> none  [the longest x24 30.7 us: update_block(): w_rms = jnp.sqrt(scalar_sum[1] / n_total)]
    reduce_sum x36 -> x0, other arithmetic: 28.9 us -> none  [the longest x32 24.2 us: update_block(): upd_sq = lax.psum(jnp.sum(update * update), BOTH_AXES)]
    another operation x20 -> x0, local copies, waits for them, and re-layouts: 17.4 us -> none  [local_step(): jnp.stack([res_item[out_idx] for res_item in results])]
  transfers between devices with their start and end apart: 1 -> 0, of which waited for: 0 -> 0; matrix products, arithmetic and copies ran while one was open for 18% -> 0% of each run, Pallas kernels for 0% -> 0%
where the time goes in v1:
time: 71 us; the launch traced here: 70.1 us
  Pallas kernels  63.2 us (89%)
  local copies, waits for them, and re-layouts  6.26 us (9%)
    pallas_call x1, Pallas kernels, local_step(): pl.pallas_call(functools.partial(kernel, dims), out_shape=(shape(layers,...  63.2 us
    unnamed x16, local copies, waits for them, and re-layouts  6.26 us

profile of v1, /device:TPU:1, one launch (start us, length us, event | category | flops | bytes accessed | tf_op | source)
XLA Modules:
  0.0 70.1 jit_solution(17418296142667711923)
XLA Ops:
  0.6 63.2 %adafactor_step.1 = (f32[16,16,1408]{2,1,0:T(8,128)}, f32[16,16]{1,0:T(8,128)}, f32[16,1408]{1,0:T(8,128)}, f32[16,16,1408]{2,1,0:T(8,128)}, f32[16,1408]{1,0:T(8,128)}, /*index=5*/f32[16,16]{1,0:T(8,128)}) custom-call(f32[3]{0:T(128)} %hyper.1, bf16[16,16,1024]{2,1,0:T(8,128)(2,1)} %bitcast.6, bf16[16,1024,1408]{2,1,0:T(8,128)(2,1)} %b_in.1, ...), custom_call_target="tpu_custom_call" | custom-call | tf_op jit(solution)/shard_map/adafactor_step/pallas_call | solution.py:304
  63.8 0.0 copy-start.4
  63.8 0.0 copy-start.2
  63.9 0.0 copy-start
  63.9 2.7 %copy.23 = f32[16,16,1408]{2,1,0:T(8,128)} copy(f32[16,16,1408]{2,1,0:T(8,128)} %get-tuple-element.24) | data formatting | bytes 2883584
  66.5 0.0 copy-done.4
  66.5 0.6 copy.24
  67.1 0.0 copy-done.2
  67.1 0.6 copy.25
  67.8 0.0 copy-done
  67.8 0.0 copy-start.1
  67.8 0.0 copy-start.3
  67.8 1.1 %copy.26 = f32[16,1408,16]{1,2,0:T(8,128)} copy(f32[16,1408,16]{1,2,0:T(8,128)S(1)} %bitcast.4) | data formatting | bytes 2883584
  68.9 0.0 copy-done.1
  68.9 0.6 copy.27
  69.5 0.0 copy-done.3
  69.5 0.6 copy.28
Async XLA Ops:
  63.8 2.7 %copy-start.4 = (f32[16,16]{1,0:T(8,128)S(1)}, f32[16,16]{1,0:T(8,128)}, u32[]{:S(2)}) copy-start(f32[16,16]{1,0:T(8,128)} %get-tuple-element.25) | copy-start | bytes 3076
  63.8 3.3 %copy-start.2 = (f32[16,1408]{1,0:T(8,128)S(1)}, f32[16,1408]{1,0:T(8,128)}, u32[]{:S(2)}) copy-start(f32[16,1408]{1,0:T(8,128)} %get-tuple-element.26) | copy-start | bytes 270340
  63.9 3.9 %copy-start = (f32[16,16,1408]{2,1,0:T(8,128)S(1)}, f32[16,16,1408]{2,1,0:T(8,128)}, u32[]{:S(2)}) copy-start(f32[16,16,1408]{2,1,0:T(8,128)} %get-tuple-element.15) | copy-start | bytes 4325380
  67.8 1.1 %copy-start.1 = (f32[16,1408]{1,0:T(8,128)S(1)}, f32[16,1408]{1,0:T(8,128)}, u32[]{:S(2)}) copy-start(f32[16,1408]{1,0:T(8,128)} %get-tuple-element.28) | copy-start | bytes 270340
  67.8 1.7 %copy-start.3 = (f32[16,16]{1,0:T(8,128)S(1)}, f32[16,16]{1,0:T(8,128)}, u32[]{:S(2)}) copy-start(f32[16,16]{1,0:T(8,128)} %get-tuple-element.29) | copy-start | bytes 3076

commit v2 on v1

v2 whole, which is shorter than its diff:
```python
import functools

import jax
import jax.numpy as jnp
from jax import lax
from jax.experimental import pallas as pl
from jax.experimental.pallas import tpu as pltpu
from jax.sharding import PartitionSpec as P

EPS_ONE = 1e-30
EPS_TWO = 1e-3
MESH = pl.DeviceIdType.MESH
LANES = 128
SLOTS = 8
LAG = 3
VMEM_LIMIT = 48 * 1024 * 1024


def torus_dims(n_row):
    side = round(n_row ** (1.0 / 3.0))
    return side, side, side


def kernel(dims, hyper, a_in, b_in, w_in, side_in, lane_in, a_out, b_out, w_out, lane_out, side_out,
           w_v, side_res, lane_res,
           hyper_s, a_v, b_v, g_v, side_old, lane_old, old_pack, side_new,
           fac_v, new_pack, u_v, pair_buf, x_buf, y_buf, z_buf, fin_buf,
           load_sem, b_sem, send_sem, pair_sem, x_sem, y_sem, z_sem, fin_sem):
    nz, ny, nx = dims
    layers, depth, width = w_in.shape
    chunks = width // LANES
    n_row = nz * ny * nx
    n_side = float(depth * n_row)
    n_lane = float(width * 2)
    n_total = n_side * n_lane
    half = u_v.shape[1]

    row = lax.axis_index("row")
    core = lax.axis_index("col")
    my_x = lax.rem(row, nx)
    my_y = lax.rem(row // nx, ny)
    my_z = row // (nx * ny)

    def dev(z, y, x, c):
        return {"row": (z * ny + y) * nx + x, "col": c}

    x_devs = [dev(my_z, my_y, lax.rem(my_x + d, nx), core) for d in range(1, nx)]
    y_devs = [dev(my_z, lax.rem(my_y + d, ny), my_x, core) for d in range(1, ny)]
    z_devs = [dev(lax.rem(my_z + d, nz), my_y, my_x, core) for d in range(1, nz)]
    partner = dev(my_z, my_y, my_x, 1 - core)

    b_refs = (b_in, b_out)

    def b_copy(layer, j):
        slot = lax.rem(2 * layer + j, SLOTS)
        return pltpu.make_async_copy(b_refs[j].at[layer], b_v.at[slot], b_sem.at[slot])

    small = [(hyper, hyper_s), (a_in, a_v.at[0]), (a_out, a_v.at[1]), (side_in, side_old.at[0]), (side_out, side_old.at[1]),
             (lane_in, lane_old.at[0]), (lane_out, lane_old.at[1])]
    small = [pltpu.make_async_copy(s, d, load_sem.at[i]) for i, (s, d) in enumerate(small)]
    big = [pltpu.make_async_copy(s, w_v.at[j], load_sem.at[len(small) + j]) for j, s in enumerate((w_in, w_out))]
    for c in small:
        c.start()
    for s in range(SLOTS):
        b_copy(s // 2, s % 2).start()
        if s == 3:
            for c in big:
                c.start()

    barrier = pltpu.get_barrier_semaphore()
    peers = x_devs + y_devs + z_devs + [partner]
    for d in peers:
        pl.semaphore_signal(barrier, inc=1, device_id=d, device_id_type=MESH)
    for c in small:
        c.wait()

    beta = hyper_s[0]
    keep = 1.0 - beta
    eye = lax.broadcasted_iota(jnp.int32, (depth, depth), 0) == lax.broadcasted_iota(jnp.int32, (depth, depth), 1)
    half_id = lax.broadcasted_iota(jnp.int32, (half, LANES), 0)
    first = half_id < chunks
    second = (half_id >= chunks) & (half_id < 2 * chunks)

    for layer in range(layers):
        for j in range(2):
            for k in range(chunks):
                old_pack[layer, j * chunks + k:j * chunks + k + 1, :] = lane_old[j, layer:layer + 1, k * LANES:(k + 1) * LANES]
            line = jnp.broadcast_to(side_old[j, layer:layer + 1, :], (depth, depth))
            line = jnp.sum(jnp.where(eye, line, 0.0), axis=1, keepdims=True)
            side_new[layer, j * depth:(j + 1) * depth, :] = jnp.broadcast_to(line, (depth, LANES))
        old_pack[layer, 2 * chunks:, :] = jnp.ones((half - 2 * chunks, LANES), jnp.float32)
        line = jnp.sum(jnp.where(second, old_pack[layer], 0.0), axis=0, keepdims=True)
        pair_buf[layer, core, 2 * depth:, :] = jnp.broadcast_to(line, (8, LANES))
    pl.semaphore_wait(barrier, len(peers))

    def send(ref, recv, d, k):
        pltpu.make_async_remote_copy(src_ref=ref, dst_ref=ref, send_sem=send_sem.at[k], recv_sem=recv, device_id=d, device_id_type=MESH).start()

    def arrived(ref, sem):
        pltpu.make_async_copy(ref, ref, sem).wait()

    def total(buf, layer, count):
        out = buf[layer, 0]
        for s in range(1, count):
            out = out + buf[layer, s]
        return out

    def stage_a(layer):
        for j in range(2):
            b_copy(layer, j).wait()
            slot = lax.rem(2 * layer + j, SLOTS)
            grad = jnp.dot(a_v[j, layer], b_v[slot], preferred_element_type=jnp.float32)
            nxt = layer + SLOTS // 2

            @pl.when(nxt < layers)
            def _():
                b_copy(nxt, j).start()

            g_v[j, layer] = grad
            sq = grad * grad + EPS_ONE
            lane_part = jnp.sum(sq, axis=0, keepdims=True)
            side_part = sq[:, :LANES]
            for k in range(chunks):
                cols = slice(k * LANES, (k + 1) * LANES)
                if k:
                    side_part = side_part + sq[:, cols]
                x_buf[layer, my_x, j * chunks + k:j * chunks + k + 1, :] = lane_part[:, cols]
            pair_buf[layer, core, j * depth:(j + 1) * depth, :] = side_part
        send(pair_buf.at[layer, core], pair_sem.at[layer], partner, 0)

    def stage_d(layer):
        arrived(pair_buf.at[layer, 0], pair_sem.at[layer])
        both = total(pair_buf, layer, 2)
        side_sum = jnp.sum(both[:2 * depth], axis=1, keepdims=True)
        new = beta * side_new[layer] + side_sum * (keep / n_lane)
        side_new[layer] = new
        inv = lax.rsqrt(new)
        for j in range(2):
            fac = inv[j * depth:(j + 1) * depth]
            w_sq = None
            for k in range(chunks):
                cols = slice(k * LANES, (k + 1) * LANES)
                upd = g_v[j, layer, :, cols] * fac
                g_v[j, layer, :, cols] = upd
                x_buf[layer, my_x, half + j * chunks + k:half + j * chunks + k + 1, :] = jnp.sum(upd * upd, axis=0, keepdims=True)
                wgt = w_v[j, layer, :, cols]
                w_sq = wgt * wgt if k == 0 else w_sq + wgt * wgt
            x_buf[layer, my_x, half + 2 * chunks + j:half + 2 * chunks + j + 1, :] = jnp.sum(w_sq, axis=0, keepdims=True)
        mean_in = jnp.sum(new[:depth], axis=0, keepdims=True) * (1.0 / (n_side * LANES))
        mean_out = jnp.broadcast_to(jnp.sum(side_sum[depth:], axis=0, keepdims=True), (1, LANES)) * (keep / (n_total * LANES))
        mean_out = mean_out + both[2 * depth:2 * depth + 1] * (beta / (n_lane * n_row))
        x_buf[layer, my_x, 2 * chunks:2 * chunks + 1, :] = mean_in
        x_buf[layer, my_x, 2 * chunks + 1:2 * chunks + 2, :] = mean_out
        for d in x_devs:
            send(x_buf.at[layer, my_x], x_sem.at[layer], d, 1)

    def stage_x(layer):
        arrived(x_buf.at[layer, pl.ds(0, nx - 1)], x_sem.at[layer])
        y_buf[layer, my_y] = total(x_buf, layer, nx)
        for d in y_devs:
            send(y_buf.at[layer, my_y], y_sem.at[layer], d, 2)

    def stage_y(layer):
        arrived(y_buf.at[layer, pl.ds(0, ny - 1)], y_sem.at[layer])
        z_buf[layer, my_z] = total(y_buf, layer, ny)
        for d in z_devs:
            send(z_buf.at[layer, my_z], z_sem.at[layer], d, 3)

    def stage_z(layer):
        arrived(z_buf.at[layer, pl.ds(0, nz - 1)], z_sem.at[layer])
        tot = total(z_buf, layer, nz)
        low, high = tot[:half], tot[half:]
        new = beta * old_pack[layer] + low * (keep / n_side)
        new_pack[layer] = new
        mean = jnp.sqrt(jnp.sum(low[2 * chunks:2 * chunks + 2, :], axis=1, keepdims=True))
        u = lax.rsqrt(new) * jnp.where(first, mean[0:1], mean[1:2])
        u_v[layer] = u
        part = (high * u) * u
        fin_buf[layer, core, 0:1, :] = jnp.sum(jnp.where(first, part, 0.0), axis=0, keepdims=True)
        fin_buf[layer, core, 1:2, :] = jnp.sum(jnp.where(second, part, 0.0), axis=0, keepdims=True)
        fin_buf[layer, core, 2:4, :] = high[2 * chunks:2 * chunks + 2, :]
        fin_buf[layer, core, 4:, :] = jnp.zeros((4, LANES), jnp.float32)
        send(fin_buf.at[layer, core], fin_sem.at[layer], partner, 4)

    def stage_f(layer):
        arrived(fin_buf.at[layer, 0], fin_sem.at[layer])
        rms = jnp.sqrt(jnp.sum(total(fin_buf, layer, 2), axis=1, keepdims=True) / n_total)
        amount = hyper_s[1] * jnp.maximum(EPS_TWO, rms[2:4]) / jnp.maximum(1.0, rms[0:2] / hyper_s[2])
        fac_v[...] = u_v[layer] * jnp.where(first, amount[0:1], amount[1:2])
        for j in range(2):
            for k in range(chunks):
                cols = slice(k * LANES, (k + 1) * LANES)
                w_v[j, layer, :, cols] = w_v[j, layer, :, cols] - g_v[j, layer, :, cols] * fac_v[j * chunks + k:j * chunks + k + 1, :]

    def at(i, lag, stage, count):
        pl.when((i >= lag) & (i < count + lag))(lambda: stage(i - lag))

    def step(i, carry):
        at(i, 0, stage_a, layers)

        @pl.when(i == 1)
        def _():
            for c in big:
                c.wait()

        at(i, 1, stage_d, layers)
        at(i, 1 + LAG, stage_x, layers)
        at(i, 1 + 2 * LAG, stage_y, layers)
        at(i, 1 + 3 * LAG, stage_z, layers)
        at(i, 2 + 3 * LAG, stage_f, layers - 1)
        return carry

    lax.fori_loop(0, layers + 1 + 3 * LAG, step, 0)

    for layer in range(layers):
        for j in range(2):
            for k in range(chunks):
                lane_res[j, layer:layer + 1, k * LANES:(k + 1) * LANES] = new_pack[layer, j * chunks + k:j * chunks + k + 1, :]
            line = side_new[layer, j * depth:(j + 1) * depth, :depth]
            side_res[j, layer:layer + 1, :] = jnp.sum(jnp.where(eye, line, 0.0), axis=0, keepdims=True)
    stage_f(layers - 1)

    def sent(ref, k):
        pltpu.make_async_copy(ref, ref, send_sem.at[k]).wait()

    sent(pair_buf.at[:, 0], 0)
    sent(x_buf.at[:, pl.ds(0, nx - 1)], 1)
    sent(y_buf.at[:, pl.ds(0, ny - 1)], 2)
    sent(z_buf.at[:, pl.ds(0, nz - 1)], 3)
    sent(fin_buf.at[:, 0], 4)


def write_kernel(w_v, side_v, lane_v, o_w_in, o_side_in, o_lane_in, o_w_out, o_lane_out, o_side_out, sem):
    pairs = [(w_v.at[0], o_w_in), (w_v.at[1], o_w_out), (lane_v.at[0], o_lane_in), (lane_v.at[1], o_lane_out), (side_v.at[0], o_side_in), (side_v.at[1], o_side_out)]
    copies = [pltpu.make_async_copy(s, d, sem.at[i]) for i, (s, d) in enumerate(pairs)]
    for c in copies:
        c.start()
    for c in copies:
        c.wait()


def solution(mesh):
    dims = torus_dims(mesh.shape['row'])
    nz, ny, nx = dims
    tile_in = P(None, 'row', 'col')
    tile_out = P(None, 'col', 'row')
    lane_row = P(None, None, 'row')
    lane_col = P(None, None, 'col')
    vec_row = P(None, 'row')
    vec_col = P(None, 'col')

    def local_step(hyper_params, w_in, x_in, dy_in, row_in, col_in, w_out, x_out, dy_out, row_out, col_out):
        layers, depth, width = w_in.shape
        tokens = x_in.shape[1]
        chunks = width // LANES
        half = -(-(2 * chunks + 2) // 8) * 8
        f32 = jnp.float32
        turn = lambda v: jnp.swapaxes(v, 1, 2)
        vm = pltpu.VMEM
        dma = pltpu.SemaphoreType.DMA
        scratch = [
            pltpu.SMEM((3,), f32), vm((2, layers, depth, tokens), jnp.bfloat16), vm((SLOTS, tokens, width), jnp.bfloat16),
            vm((2, layers, depth, width), f32), vm((2, layers, depth), f32), vm((2, layers, width), f32),
            vm((layers, half, LANES), f32), vm((layers, 2 * depth, LANES), f32), vm((half, LANES), f32), vm((layers, half, LANES), f32), vm((layers, half, LANES), f32),
            vm((layers, 2, 2 * depth + 8, LANES), f32),
            vm((layers, nx, 2 * half, LANES), f32), vm((layers, ny, 2 * half, LANES), f32), vm((layers, nz, 2 * half, LANES), f32), vm((layers, 2, 8, LANES), f32),
            dma((9,)), dma((SLOTS,)), dma((5,)), dma((layers,)), dma((layers,)), dma((layers,)), dma((layers,)), dma((layers,)),
        ]
        in_vmem = pl.BlockSpec(memory_space=vm)
        anywhere = pl.BlockSpec(memory_space=pl.ANY)
        held = pl.pallas_call(
            functools.partial(kernel, dims),
            out_shape=(vm((2, layers, depth, width), f32), vm((2, layers, depth), f32), vm((2, layers, width), f32)),
            in_specs=[pl.BlockSpec(memory_space=pltpu.HBM)] * 11,
            out_specs=[in_vmem] * 3,
            scratch_shapes=scratch,
            name="adafactor_step",
            compiler_params=pltpu.CompilerParams(collective_id=0, has_side_effects=True, vmem_limit_bytes=VMEM_LIMIT),
        )(*[pltpu.with_memory_space_constraint(v, pltpu.HBM) for v in (hyper_params, turn(x_in), dy_in, w_in, row_in, col_in, turn(dy_out), x_out, turn(w_out), row_out, col_out)])
        shape = lambda *s: jax.ShapeDtypeStruct(s, f32)
        res = pl.pallas_call(
            write_kernel,
            out_shape=(shape(layers, depth, width), shape(layers, depth), shape(layers, width), shape(layers, depth, width), shape(layers, width), shape(layers, depth)),
            in_specs=[anywhere] * 3,
            out_specs=[anywhere] * 6,
            scratch_shapes=[dma((6,))],
            name="write_back",
            compiler_params=pltpu.CompilerParams(vmem_limit_bytes=4 * 1024 * 1024),
        )(*held)
        return res[0], res[1], res[2], turn(res[3]), res[4], res[5]

    return jax.shard_map(local_step, mesh=mesh, in_specs=(P(), tile_in, lane_row, lane_col, vec_row, vec_col, tile_out, lane_col, lane_row, vec_col, vec_row), out_specs=(tile_in, vec_row, vec_col, tile_out, vec_col, vec_row), check_vma=False)
```

time: 71 us -> 52.8 us (0.74); the launches traced: 70.1 us -> 52.7 us
  Pallas kernels: 63.2 us -> 52 us
  local copies, waits for them, and re-layouts: 6.26 us -> 0 us
    pallas_call x1 -> x2, Pallas kernels: 63.2 us -> 52 us  [the longest x1 50.4 us: local_step(): pl.pallas_call(functools.partial(kernel, dims), out_shape=(vm((2, layers,...]
    unnamed x16 -> x0, local copies, waits for them, and re-layouts: 6.26 us -> none
where the time goes in v2:
time: 52.8 us; the launch traced here: 52.7 us
  Pallas kernels  52 us (98%)
  between operations  0.64 us (1%)
    pallas_call x1, Pallas kernels, local_step(): pl.pallas_call(functools.partial(kernel, dims), out_shape=(vm((2, layers,...  50.4 us
    pallas_call x1, Pallas kernels, local_step(): pl.pallas_call(write_kernel, out_shape=(shape(layers, depth, width), shap...  1.68 us

profile of v2, /device:TPU:1, one launch (start us, length us, event | category | flops | bytes accessed | tf_op | source)
XLA Modules:
  0.0 52.7 jit_solution(3855750135369437275)
XLA Ops:
  0.6 50.4 %adafactor_step.1 = (f32[2,16,16,1408]{3,2,1,0:T(8,128)S(1)}, f32[2,16,16]{2,1,0:T(8,128)S(1)}, f32[2,16,1408]{2,1,0:T(8,128)S(1)}) custom-call(f32[3]{0:T(128)} %hyper.1, bf16[16,16,1024]{2,1,0:T(8,128)(2,1)} %bitcast.5, bf16[16,1024,1408]{2,1,0:T(8,128)(2,1)} %b_in.1, f32[16,16,1408]{2,1,0:T(8,128)} %w_in.1, f32[16,16]{1,0:T(8,128)} %side_in.1, ...), custom_call_target="tpu_custom_call" | custom-call | tf_op jit(solution)/shard_map/adafactor_step/pallas_call | solution.py:271
  51.0 1.7 %write_back.1 = (f32[16,16,1408]{2,1,0:T(8,128)}, f32[16,16]{1,0:T(8,128)}, f32[16,1408]{1,0:T(8,128)}, f32[16,16,1408]{2,1,0:T(8,128)}, f32[16,1408]{1,0:T(8,128)}, /*index=5*/f32[16,16]{1,0:T(8,128)}) custom-call(f32[2,16,16,1408]{3,2,1,0:T(8,128)S(1)} %get-tuple-element.15.w_v, f32[2,16,16]{2,1,0:T(8,128)S(1)} %get-tuple-element.16.side_v, ...), custom_call_target="tpu_custom_call" | custom-call | tf_op jit(solution)/shard_map/write_back/pallas_call | solution.py:281

commit v3 on v0

v3 whole, which is shorter than its diff:
```python
import functools

import jax
import jax.numpy as jnp
from jax import lax
from jax.experimental import pallas as pl
from jax.experimental.pallas import tpu as pltpu
from jax.sharding import PartitionSpec as P

EPS_ONE = 1e-30
EPS_TWO = 1e-3
MESH = pl.DeviceIdType.MESH
LANES = 128
SLOTS = 8
LAG = 5
LAG_D = 3
VMEM_LIMIT = 48 * 1024 * 1024


def torus_side(n_row):
    return round(n_row ** (1.0 / 3.0))


def kernel(side, hyper, a_in, b_in, w_in, side_in, lane_in, a_out, b_out, w_out, lane_out, side_out,
           w_v, side_res, lane_res,
           hyper_s, a_v, b_v, g_v, r_v, side_old, lane_old, old_pack, side_buf, side_out_buf, side_back,
           fac_v, new_pack, u_v, pair_buf, p_buf, fin_buf,
           load_sem, a_sem, ar_sem, b_sem, send_sem, so_sem, sb_sem, pair_sem, p_sem, g_sem, fin_sem):
    layers, depth, width = w_in.shape
    chunks = width // LANES
    half = chunks + 1
    n_row = side ** 3
    n_side = float(depth * n_row)
    n_lane = float(width * 2)
    n_total = n_side * n_lane

    row = lax.axis_index("row")
    core = lax.axis_index("col")

    def stride_of(d):
        return 1 + (side - 1) * d + ((side - 1) * (side - 1) * d * (d - 1)) // 2

    def pos_of(d):
        return lax.rem(row // stride_of(d), side)

    def moved(d, pos):
        return row + (pos - pos_of(d)) * stride_of(d)

    def pair(layer):
        kind = lax.rem(layer, 6)
        d = kind // 2
        flavour = lax.rem(kind, 2)
        pos = pos_of(d)
        role = lax.rem(pos, 2)
        mate = lax.rem(pos + (1 - 2 * role) * (1 - 2 * flavour) + side, side)
        return d, role, moved(d, mate)

    def dev(r, c):
        return {"row": r, "col": c}

    b_refs = (b_in, b_out)
    a_refs = (a_in, a_out)

    def b_start(layer):
        slot = lax.rem(layer, SLOTS)
        role = pair(layer)[1]
        for j in range(2):
            @pl.when(role == j)
            def _():
                pltpu.make_async_copy(b_refs[j].at[layer], b_v.at[slot], b_sem.at[slot]).start()

    small = [(hyper, hyper_s), (side_in, side_old.at[0]), (side_out, side_old.at[1]), (lane_in, lane_old.at[0]), (lane_out, lane_old.at[1])]
    small = [pltpu.make_async_copy(s, d, load_sem.at[i]) for i, (s, d) in enumerate(small)]
    big = [pltpu.make_async_copy(s, w_v.at[j], load_sem.at[len(small) + j]) for j, s in enumerate((w_in, w_out))]
    barrier = pltpu.get_barrier_semaphore()
    peers = [dev(moved(d, lax.rem(pos_of(d) + t, side)), core) for d in range(3) for t in range(1, side)] + [dev(row, 1 - core)]
    for d in peers:
        pl.semaphore_signal(barrier, inc=1, device_id=d, device_id_type=MESH)
    for c in small:
        c.start()

    def load_a(layer, carry):
        role = pair(layer)[1]
        for j in range(2):
            @pl.when(role == j)
            def _():
                pltpu.make_async_copy(a_refs[j].at[layer], a_v.at[layer, pl.ds(0, depth)], a_sem.at[layer]).start()
        return carry

    lax.fori_loop(0, layers, load_a, 0)
    for s in range(SLOTS):
        b_start(s)
        if s == 3:
            for c in big:
                c.start()
    for c in small:
        c.wait()

    beta = hyper_s[0]
    keep = 1.0 - beta
    eye = lax.broadcasted_iota(jnp.int32, (depth, depth), 0) == lax.broadcasted_iota(jnp.int32, (depth, depth), 1)
    half_id = lax.broadcasted_iota(jnp.int32, (half, LANES), 0)
    real = half_id < chunks
    left = lax.broadcasted_iota(jnp.int32, (1, LANES), 1) < LANES // 2

    def send(src, dst, recv, d, k):
        pltpu.make_async_remote_copy(src_ref=src, dst_ref=dst, send_sem=send_sem.at[k], recv_sem=recv, device_id=d, device_id_type=MESH).start()

    def arrived(ref, sem):
        pltpu.make_async_copy(ref, ref, sem).wait()

    pl.semaphore_wait(barrier, len(peers))

    def send_a(layer, carry):
        _, role, mate = pair(layer)
        for j in range(2):
            @pl.when(role == 1 - j)
            def _():
                send(a_refs[j].at[layer], a_v.at[layer, pl.ds(depth, depth)], ar_sem.at[layer], dev(mate, core), 0)
        return carry

    lax.fori_loop(0, layers, send_a, 0)

    for layer in range(layers):
        _, role, mate = pair(layer)
        column = []
        for j in range(2):
            for k in range(chunks):
                old_pack[layer, j, k:k + 1, :] = lane_old[j, layer:layer + 1, k * LANES:(k + 1) * LANES]
            old_pack[layer, j, chunks:, :] = jnp.ones((half - chunks, LANES), jnp.float32)
            line = jnp.broadcast_to(side_old[j, layer:layer + 1, :], (depth, depth))
            line = jnp.sum(jnp.where(eye, line, 0.0), axis=1, keepdims=True)
            column.append(jnp.broadcast_to(line, (depth, LANES)))
        side_buf[layer, :depth, :] = jnp.where(role == 0, column[0], column[1])
        side_out_buf[layer] = jnp.where(role == 0, column[1], column[0])
        send(side_out_buf.at[layer], side_buf.at[layer, pl.ds(depth, depth)], so_sem.at[layer], dev(mate, core), 1)
        line = jnp.sum(jnp.where(real, old_pack[layer, 1], 0.0), axis=0, keepdims=True)
        pair_buf[layer, core, 2 * depth:, :] = jnp.broadcast_to(line, (8, LANES))

    def stage_a(layer):
        d, role, mate = pair(layer)
        mine = p_buf.at[0, layer, pos_of(lax.rem(d + 1, 3))]
        slot = lax.rem(layer, SLOTS)
        arrived(a_v.at[layer, pl.ds(0, depth)], a_sem.at[layer])
        arrived(a_v.at[layer, pl.ds(0, depth)], ar_sem.at[layer])
        arrived(b_v.at[slot], b_sem.at[slot])
        grad = jnp.dot(a_v[layer], b_v[slot], preferred_element_type=jnp.float32)
        g_v[layer] = grad
        sq = grad * grad + EPS_ONE
        lane_part = jnp.sum(sq, axis=0, keepdims=True)
        part = sq[:, :LANES]
        for k in range(chunks):
            cols = slice(k * LANES, (k + 1) * LANES)
            if k:
                part = part + sq[:, cols]
            mine[k:k + 1, :] = lane_part[:, cols]
        pair_buf[layer, core, :2 * depth, :] = part
        send(pair_buf.at[layer, core], pair_buf.at[layer, core], pair_sem.at[layer], dev(row, 1 - core), 2)
        pl.when(layer + SLOTS < layers)(lambda: b_start(layer + SLOTS))

    def total(buf, count):
        out = buf[0]
        for s in range(1, count):
            out = out + buf[s]
        return out

    def stage_d(layer):
        d, role, mate = pair(layer)
        arrived(side_buf.at[layer, pl.ds(0, depth)], so_sem.at[layer])
        arrived(pair_buf.at[layer, 0], pair_sem.at[layer])
        both = total(pair_buf.at[layer], 2)
        side_sum = jnp.sum(both[:2 * depth], axis=1, keepdims=True)
        new = beta * side_buf[layer] + side_sum * (keep / n_lane)
        side_buf[layer] = new
        inv = lax.rsqrt(new)
        axis = lax.rem(d + 1, 3)
        me = pos_of(axis)
        mine = p_buf.at[0, layer, me]
        for k in range(chunks):
            cols = slice(k * LANES, (k + 1) * LANES)
            upd = g_v[layer, :, cols] * inv
            g_v[layer, :, cols] = upd
            mine[half + k:half + k + 1, :] = jnp.sum(upd * upd, axis=0, keepdims=True)
        w_sum = []
        for j in range(2):
            w_sq = None
            for k in range(chunks):
                wgt = w_v[j, layer, :, k * LANES:(k + 1) * LANES]
                w_sq = wgt * wgt if k == 0 else w_sq + wgt * wgt
            w_sum.append(jnp.sum(jnp.sum(w_sq, axis=0, keepdims=True), axis=1, keepdims=True) * (2.0 / LANES))
        mine[2 * half - 1:2 * half, :] = jnp.where(left, w_sum[0], w_sum[1])
        mean_in = jnp.sum(new, axis=0, keepdims=True) * (1.0 / (n_side * LANES))
        mean_out = jnp.broadcast_to(jnp.sum(side_sum, axis=0, keepdims=True), (1, LANES)) * (keep / (n_total * LANES))
        mean_out = mean_out + both[2 * depth:2 * depth + 1] * (beta / (n_lane * (n_row // 2)))
        mine[chunks:half, :] = jnp.where(role == 0, mean_in, mean_out)
        for t in range(1, side):
            send(mine, mine, p_sem.at[0, layer], dev(moved(axis, lax.rem(me + t, side)), core), 3)
        send(g_v.at[layer, pl.ds(depth, depth)], r_v.at[layer], g_sem.at[layer], dev(mate, core), 4)
        send(side_buf.at[layer, pl.ds(depth, depth)], side_back.at[layer], sb_sem.at[layer], dev(mate, core), 5)

    def stage_p(step, layer):
        arrived(p_buf.at[step, layer, pl.ds(0, side - 1)], p_sem.at[step, layer])
        axis = lax.rem(pair(layer)[0] + step + 2, 3)
        me = pos_of(axis)
        mine = p_buf.at[step + 1, layer, me]
        mine[...] = total(p_buf.at[step, layer], side)
        for t in range(1, side):
            send(mine, mine, p_sem.at[step + 1, layer], dev(moved(axis, lax.rem(me + t, side)), core), 6 + step)

    def stage_z(layer):
        arrived(p_buf.at[2, layer, pl.ds(0, side - 1)], p_sem.at[2, layer])
        weights = None
        for j in range(2):
            low = p_buf[2, layer, j, :half]
            high = p_buf[2, layer, j, half:]
            for s in range(j + 2, side, 2):
                low = low + p_buf[2, layer, s, :half]
                high = high + p_buf[2, layer, s, half:]
            new = jnp.where(real, beta * old_pack[layer, j] + low * (keep / n_side), 1.0)
            new_pack[layer, j] = new
            mean = jnp.sum(low[chunks:half], axis=1, keepdims=True)
            u = lax.rsqrt(new) * jnp.sqrt(mean)
            u_v[layer, j] = u
            fin_buf[layer, core, j:j + 1, :] = jnp.sum(jnp.where(real, (high * u) * u, 0.0), axis=0, keepdims=True)
            weights = high[half - 1:half] if j == 0 else weights + high[half - 1:half]
        fin_buf[layer, core, 2:3, :] = jnp.where(left, weights, 0.0)
        fin_buf[layer, core, 3:4, :] = jnp.where(left, 0.0, weights)
        fin_buf[layer, core, 4:, :] = jnp.zeros((4, LANES), jnp.float32)
        send(fin_buf.at[layer, core], fin_buf.at[layer, core], fin_sem.at[layer], dev(row, 1 - core), 8)

    def stage_f(layer):
        role = pair(layer)[1]
        arrived(r_v.at[layer], g_sem.at[layer])
        arrived(fin_buf.at[layer, 0], fin_sem.at[layer])
        rms = jnp.sqrt(jnp.sum(total(fin_buf.at[layer], 2), axis=1, keepdims=True) / n_total)
        amount = hyper_s[1] * jnp.maximum(EPS_TWO, rms[2:4]) / jnp.maximum(1.0, rms[0:2] / hyper_s[2])
        for j in range(2):
            fac_v[j] = u_v[layer, j] * amount[j:j + 1]
        for k in range(chunks):
            cols = slice(k * LANES, (k + 1) * LANES)
            w_v[role, layer, :, cols] = w_v[role, layer, :, cols] - g_v[layer, :depth, cols] * fac_v[role, k:k + 1, :]
            w_v[1 - role, layer, :, cols] = w_v[1 - role, layer, :, cols] - r_v[layer, :, cols] * fac_v[1 - role, k:k + 1, :]

    def at(i, lag, stage, count):
        pl.when((i >= lag) & (i < count + lag))(lambda: stage(i - lag))

    lag_z = LAG_D + 3 * LAG

    def step(i, carry):
        at(i, 0, stage_a, layers)

        @pl.when(i == LAG_D)
        def _():
            for c in big:
                c.wait()

        at(i, LAG_D, stage_d, layers)
        at(i, LAG_D + LAG, functools.partial(stage_p, 0), layers)
        at(i, LAG_D + 2 * LAG, functools.partial(stage_p, 1), layers)
        at(i, lag_z, stage_z, layers)
        at(i, lag_z + 1, stage_f, layers - 1)
        return carry

    lax.fori_loop(0, layers + lag_z, step, 0)

    for layer in range(layers):
        role = pair(layer)[1]
        arrived(side_back.at[layer], sb_sem.at[layer])
        for j in range(2):
            for k in range(chunks):
                lane_res[j, layer:layer + 1, k * LANES:(k + 1) * LANES] = new_pack[layer, j, k:k + 1, :]
        side_res[role, layer:layer + 1, :] = jnp.sum(jnp.where(eye, side_buf[layer, :depth, :depth], 0.0), axis=0, keepdims=True)
        side_res[1 - role, layer:layer + 1, :] = jnp.sum(jnp.where(eye, side_back[layer, :, :depth], 0.0), axis=0, keepdims=True)
    stage_f(layers - 1)

    def sent(ref, k):
        pltpu.make_async_copy(ref, ref, send_sem.at[k]).wait()

    sent(a_v.at[:, pl.ds(0, depth)], 0)
    sent(side_out_buf, 1)
    sent(pair_buf.at[:, 0], 2)
    sent(p_buf.at[0, :, pl.ds(0, side - 1)], 3)
    sent(r_v, 4)
    sent(side_back, 5)
    sent(p_buf.at[1, :, pl.ds(0, side - 1)], 6)
    sent(p_buf.at[2, :, pl.ds(0, side - 1)], 7)
    sent(fin_buf.at[:, 0], 8)


def write_kernel(w_v, side_v, lane_v, o_w_in, o_side_in, o_lane_in, o_w_out, o_lane_out, o_side_out, sem):
    pairs = [(w_v.at[0], o_w_in), (w_v.at[1], o_w_out), (lane_v.at[0], o_lane_in), (lane_v.at[1], o_lane_out), (side_v.at[0], o_side_in), (side_v.at[1], o_side_out)]
    copies = [pltpu.make_async_copy(s, d, sem.at[i]) for i, (s, d) in enumerate(pairs)]
    for c in copies:
        c.start()
    for c in copies:
        c.wait()


def solution(mesh):
    side = torus_side(mesh.shape['row'])
    tile_in = P(None, 'row', 'col')
    tile_out = P(None, 'col', 'row')
    lane_row = P(None, None, 'row')
    lane_col = P(None, None, 'col')
    vec_row = P(None, 'row')
    vec_col = P(None, 'col')

    def local_step(hyper_params, w_in, x_in, dy_in, row_in, col_in, w_out, x_out, dy_out, row_out, col_out):
        layers, depth, width = w_in.shape
        tokens = x_in.shape[1]
        chunks = width // LANES
        half = chunks + 1
        f32 = jnp.float32
        turn = lambda v: jnp.swapaxes(v, 1, 2)
        vm = pltpu.VMEM
        dma = pltpu.SemaphoreType.DMA
        scratch = [
            pltpu.SMEM((3,), f32), vm((layers, 2 * depth, tokens), jnp.bfloat16), vm((SLOTS, tokens, width), jnp.bfloat16),
            vm((layers, 2 * depth, width), f32), vm((layers, depth, width), f32),
            vm((2, layers, depth), f32), vm((2, layers, width), f32), vm((layers, 2, half, LANES), f32),
            vm((layers, 2 * depth, LANES), f32), vm((layers, depth, LANES), f32), vm((layers, depth, LANES), f32),
            vm((2, half, LANES), f32), vm((layers, 2, half, LANES), f32), vm((layers, 2, half, LANES), f32),
            vm((layers, 2, 2 * depth + 8, LANES), f32), vm((3, layers, side, 2 * half, LANES), f32), vm((layers, 2, 8, LANES), f32),
            dma((7,)), dma((layers,)), dma((layers,)), dma((SLOTS,)), dma((9,)), dma((layers,)), dma((layers,)), dma((layers,)), dma((3, layers)), dma((layers,)), dma((layers,)),
        ]
        in_vmem = pl.BlockSpec(memory_space=vm)
        anywhere = pl.BlockSpec(memory_space=pl.ANY)
        held = pl.pallas_call(
            functools.partial(kernel, side),
            out_shape=(vm((2, layers, depth, width), f32), vm((2, layers, depth), f32), vm((2, layers, width), f32)),
            in_specs=[pl.BlockSpec(memory_space=pltpu.HBM)] * 11,
            out_specs=[in_vmem] * 3,
            scratch_shapes=scratch,
            name="adafactor_step",
            compiler_params=pltpu.CompilerParams(collective_id=0, has_side_effects=True, vmem_limit_bytes=VMEM_LIMIT),
        )(*[pltpu.with_memory_space_constraint(v, pltpu.HBM) for v in (hyper_params, turn(x_in), dy_in, w_in, row_in, col_in, turn(dy_out), x_out, turn(w_out), row_out, col_out)])
        shape = lambda *s: jax.ShapeDtypeStruct(s, f32)
        res = pl.pallas_call(
            write_kernel,
            out_shape=(shape(layers, depth, width), shape(layers, depth), shape(layers, width), shape(layers, depth, width), shape(layers, width), shape(layers, depth)),
            in_specs=[anywhere] * 3,
            out_specs=[anywhere] * 6,
            scratch_shapes=[dma((6,))],
            name="write_back",
            compiler_params=pltpu.CompilerParams(vmem_limit_bytes=4 * 1024 * 1024),
        )(*held)
        return res[0], res[1], res[2], turn(res[3]), res[4], res[5]

    return jax.shard_map(local_step, mesh=mesh, in_specs=(P(), tile_in, lane_row, lane_col, vec_row, vec_col, tile_out, lane_col, lane_row, vec_col, vec_row), out_specs=(tile_in, vec_row, vec_col, tile_out, vec_col, vec_row), check_vma=False)
```

time: 669 us -> 47.9 us (0.07)
  between operations: 183 us -> 0.64 us
  other arithmetic: 167 us -> 0 us
  blocking collectives: 140 us -> 0 us
  matrix products: 112 us -> 0 us
  local copies, waits for them, and re-layouts: 58.8 us -> 0 us
  Pallas kernels: 0 us -> 47.1 us
    psum x3 -> x0, blocking collectives: 140 us -> none  [the longest x1 70.4 us: update_block(): scalar_sum = lax.psum(scalars, BOTH_AXES)]
    dot_general x32 -> x0, matrix products: 112 us -> none  [update_block(): lax.dot_general(x_blk, dy_blk, (((0,), (0,)), ((), ())), preferred_elemen...]
    another operation x34 -> x0, other arithmetic: 62.4 us -> none  [the longest x32 60.1 us: update_block(): jnp.stack([jnp.sum(row_part), jnp.sum(w_blk * w_blk), lead_col * jnp.sum(...]
    pallas_call x0 -> x2, Pallas kernels: none -> 47.1 us  [the longest x1 45.4 us: local_step(): pl.pallas_call(functools.partial(kernel, side), out_shape=(vm((2, layers,...]
    unnamed x30 -> x0, other arithmetic: 46.3 us -> none
    slice x25 -> x0, local copies, waits for them, and re-layouts: 31.3 us -> none  [the longest x24 30.7 us: update_block(): w_rms = jnp.sqrt(scalar_sum[1] / n_total)]
    reduce_sum x36 -> x0, other arithmetic: 28.9 us -> none  [the longest x32 24.2 us: update_block(): upd_sq = lax.psum(jnp.sum(update * update), BOTH_AXES)]
    another operation x20 -> x0, local copies, waits for them, and re-layouts: 17.4 us -> none  [local_step(): jnp.stack([res_item[out_idx] for res_item in results])]
  transfers between devices with their start and end apart: 1 -> 0, of which waited for: 0 -> 0; matrix products, arithmetic and copies ran while one was open for 18% -> 0% of each run, Pallas kernels for 0% -> 0%
where the time goes in v3:
time: 47.9 us; the launch traced here: 47.8 us
  Pallas kernels  47.1 us (98%)
  between operations  0.64 us (1%)
    pallas_call x1, Pallas kernels, local_step(): pl.pallas_call(functools.partial(kernel, side), out_shape=(vm((2, layers,...  45.4 us
    pallas_call x1, Pallas kernels, local_step(): pl.pallas_call(write_kernel, out_shape=(shape(layers, depth, width), shap...  1.68 us

profile of v3, /device:TPU:1, one launch (start us, length us, event | category | flops | bytes accessed | tf_op | source)
XLA Modules:
  0.0 47.8 jit_solution(7789814211085424243)
XLA Ops:
  0.6 45.4 %adafactor_step.1 = (f32[2,16,16,1408]{3,2,1,0:T(8,128)S(1)}, f32[2,16,16]{2,1,0:T(8,128)S(1)}, f32[2,16,1408]{2,1,0:T(8,128)S(1)}) custom-call(f32[3]{0:T(128)} %hyper.1, bf16[16,16,1024]{2,1,0:T(8,128)(2,1)} %bitcast.5, bf16[16,1024,1408]{2,1,0:T(8,128)(2,1)} %b_in.1, f32[16,16,1408]{2,1,0:T(8,128)} %w_in.1, f32[16,16]{1,0:T(8,128)} %side_in.1, ...), custom_call_target="tpu_custom_call" | custom-call | tf_op jit(solution)/shard_map/adafactor_step/pallas_call | solution.py:328
  46.1 1.7 %write_back.1 = (f32[16,16,1408]{2,1,0:T(8,128)}, f32[16,16]{1,0:T(8,128)}, f32[16,1408]{1,0:T(8,128)}, f32[16,16,1408]{2,1,0:T(8,128)}, f32[16,1408]{1,0:T(8,128)}, /*index=5*/f32[16,16]{1,0:T(8,128)}) custom-call(f32[2,16,16,1408]{3,2,1,0:T(8,128)S(1)} %get-tuple-element.15.w_v, f32[2,16,16]{2,1,0:T(8,128)S(1)} %get-tuple-element.16.side_v, ...), custom_call_target="tpu_custom_call" | custom-call | tf_op jit(solution)/shard_map/write_back/pallas_call | solution.py:338

commit v4 on v3

--- a/solution.py
+++ b/solution.py
@@ -11,9 +11,9 @@
 EPS_TWO = 1e-3
 MESH = pl.DeviceIdType.MESH
 LANES = 128
-SLOTS = 8
-LAG = 5
-LAG_D = 3
+SLOTS = 6
+LAG = 7
+LAG_D = 2
 VMEM_LIMIT = 48 * 1024 * 1024
 
 
@@ -23,9 +23,9 @@
 
 def kernel(side, hyper, a_in, b_in, w_in, side_in, lane_in, a_out, b_out, w_out, lane_out, side_out,
            w_v, side_res, lane_res,
-           hyper_s, a_v, b_v, g_v, r_v, side_old, lane_old, old_pack, side_buf, side_out_buf, side_back,
+           hyper_s, a_v, ax_v, b_v, g_v, r_v, side_old, lane_old, old_pack, side_buf, side_out_buf, side_back,
            fac_v, new_pack, u_v, pair_buf, p_buf, fin_buf,
-           load_sem, a_sem, ar_sem, b_sem, send_sem, so_sem, sb_sem, pair_sem, p_sem, g_sem, fin_sem):
+           load_sem, a_sem, ar_sem, ax_sem, w_sem, b_sem, send_sem, so_sem, sb_sem, pair_sem, p_sem, g_sem, fin_sem):
     layers, depth, width = w_in.shape
     chunks = width // LANES
     half = chunks + 1
@@ -60,6 +60,7 @@
 
     b_refs = (b_in, b_out)
     a_refs = (a_in, a_out)
+    w_refs = (w_in, w_out)
 
     def b_start(layer):
         slot = lax.rem(layer, SLOTS)
@@ -68,10 +69,10 @@
             @pl.when(role == j)
             def _():
                 pltpu.make_async_copy(b_refs[j].at[layer], b_v.at[slot], b_sem.at[slot]).start()
+            pltpu.make_async_copy(w_refs[j].at[layer], w_v.at[j, layer], w_sem.at[layer]).start()
 
     small = [(hyper, hyper_s), (side_in, side_old.at[0]), (side_out, side_old.at[1]), (lane_in, lane_old.at[0]), (lane_out, lane_old.at[1])]
     small = [pltpu.make_async_copy(s, d, load_sem.at[i]) for i, (s, d) in enumerate(small)]
-    big = [pltpu.make_async_copy(s, w_v.at[j], load_sem.at[len(small) + j]) for j, s in enumerate((w_in, w_out))]
     barrier = pltpu.get_barrier_semaphore()
     peers = [dev(moved(d, lax.rem(pos_of(d) + t, side)), core) for d in range(3) for t in range(1, side)] + [dev(row, 1 - core)]
     for d in peers:
@@ -84,15 +85,13 @@
         for j in range(2):
             @pl.when(role == j)
             def _():
+                pltpu.make_async_copy(a_refs[1 - j].at[layer], ax_v.at[layer], ax_sem.at[layer]).start()
                 pltpu.make_async_copy(a_refs[j].at[layer], a_v.at[layer, pl.ds(0, depth)], a_sem.at[layer]).start()
         return carry
 
     lax.fori_loop(0, layers, load_a, 0)
     for s in range(SLOTS):
         b_start(s)
-        if s == 3:
-            for c in big:
-                c.start()
     for c in small:
         c.wait()
 
@@ -109,41 +108,40 @@
     def arrived(ref, sem):
         pltpu.make_async_copy(ref, ref, sem).wait()
 
-    pl.semaphore_wait(barrier, len(peers))
-
-    def send_a(layer, carry):
-        _, role, mate = pair(layer)
-        for j in range(2):
-            @pl.when(role == 1 - j)
-            def _():
-                send(a_refs[j].at[layer], a_v.at[layer, pl.ds(depth, depth)], ar_sem.at[layer], dev(mate, core), 0)
-        return carry
-
-    lax.fori_loop(0, layers, send_a, 0)
-
+    old_sum = lane_old[1, :, :LANES]
+    for k in range(1, chunks):
+        old_sum = old_sum + lane_old[1, :, k * LANES:(k + 1) * LANES]
     for layer in range(layers):
-        _, role, mate = pair(layer)
+        role = pair(layer)[1]
         column = []
         for j in range(2):
-            for k in range(chunks):
-                old_pack[layer, j, k:k + 1, :] = lane_old[j, layer:layer + 1, k * LANES:(k + 1) * LANES]
-            old_pack[layer, j, chunks:, :] = jnp.ones((half - chunks, LANES), jnp.float32)
             line = jnp.broadcast_to(side_old[j, layer:layer + 1, :], (depth, depth))
             line = jnp.sum(jnp.where(eye, line, 0.0), axis=1, keepdims=True)
             column.append(jnp.broadcast_to(line, (depth, LANES)))
         side_buf[layer, :depth, :] = jnp.where(role == 0, column[0], column[1])
         side_out_buf[layer] = jnp.where(role == 0, column[1], column[0])
+        pair_buf[layer, core, 2 * depth:, :] = jnp.broadcast_to(old_sum[layer:layer + 1], (8, LANES))
+    pl.semaphore_wait(barrier, len(peers))
+
+    def send_a(layer, carry):
+        _, role, mate = pair(layer)
+        arrived(ax_v.at[layer], ax_sem.at[layer])
+        send(ax_v.at[layer], a_v.at[layer, pl.ds(depth, depth)], ar_sem.at[layer], dev(mate, core), 0)
         send(side_out_buf.at[layer], side_buf.at[layer, pl.ds(depth, depth)], so_sem.at[layer], dev(mate, core), 1)
-        line = jnp.sum(jnp.where(real, old_pack[layer, 1], 0.0), axis=0, keepdims=True)
-        pair_buf[layer, core, 2 * depth:, :] = jnp.broadcast_to(line, (8, LANES))
-
-    def stage_a(layer):
-        d, role, mate = pair(layer)
-        mine = p_buf.at[0, layer, pos_of(lax.rem(d + 1, 3))]
+        return carry
+
+    lax.fori_loop(0, layers, send_a, 0)
+
+    def wait_a(layer):
         slot = lax.rem(layer, SLOTS)
         arrived(a_v.at[layer, pl.ds(0, depth)], a_sem.at[layer])
         arrived(a_v.at[layer, pl.ds(0, depth)], ar_sem.at[layer])
         arrived(b_v.at[slot], b_sem.at[slot])
+
+    def work_a(layer):
+        d, role, mate = pair(layer)
+        mine = p_buf.at[0, layer, pos_of(lax.rem(d + 1, 3))]
+        slot = lax.rem(layer, SLOTS)
         grad = jnp.dot(a_v[layer], b_v[slot], preferred_element_type=jnp.float32)
         g_v[layer] = grad
         sq = grad * grad + EPS_ONE
@@ -155,8 +153,9 @@
                 part = part + sq[:, cols]
             mine[k:k + 1, :] = lane_part[:, cols]
         pair_buf[layer, core, :2 * depth, :] = part
+
+    def send_pair(layer):
         send(pair_buf.at[layer, core], pair_buf.at[layer, core], pair_sem.at[layer], dev(row, 1 - core), 2)
-        pl.when(layer + SLOTS < layers)(lambda: b_start(layer + SLOTS))
 
     def total(buf, count):
         out = buf[0]
@@ -164,10 +163,13 @@
             out = out + buf[s]
         return out
 
-    def stage_d(layer):
-        d, role, mate = pair(layer)
+    def wait_d(layer):
+        arrived(w_v.at[:, layer], w_sem.at[layer])
         arrived(side_buf.at[layer, pl.ds(0, depth)], so_sem.at[layer])
         arrived(pair_buf.at[layer, 0], pair_sem.at[layer])
+
+    def work_d(layer):
+        d, role, mate = pair(layer)
         both = total(pair_buf.at[layer], 2)
         side_sum = jnp.sum(both[:2 * depth], axis=1, keepdims=True)
         new = beta * side_buf[layer] + side_sum * (keep / n_lane)
@@ -193,6 +195,12 @@
         mean_out = jnp.broadcast_to(jnp.sum(side_sum, axis=0, keepdims=True), (1, LANES)) * (keep / (n_total * LANES))
         mean_out = mean_out + both[2 * depth:2 * depth + 1] * (beta / (n_lane * (n_row // 2)))
         mine[chunks:half, :] = jnp.where(role == 0, mean_in, mean_out)
+
+    def send_d(layer):
+        d, role, mate = pair(layer)
+        axis = lax.rem(d + 1, 3)
+        me = pos_of(axis)
+        mine = p_buf.at[0, layer, me]
         for t in range(1, side):
             send(mine, mine, p_sem.at[0, layer], dev(moved(axis, lax.rem(me + t, side)), core), 3)
         send(g_v.at[layer, pl.ds(depth, depth)], r_v.at[layer], g_sem.at[layer], dev(mate, core), 4)
@@ -246,22 +254,48 @@
 
     lag_z = LAG_D + 3 * LAG
 
-    def step(i, carry):
-        at(i, 0, stage_a, layers)
-
-        @pl.when(i == LAG_D)
-        def _():
-            for c in big:
-                c.wait()
-
-        at(i, LAG_D, stage_d, layers)
+    def exchange(i):
         at(i, LAG_D + LAG, functools.partial(stage_p, 0), layers)
         at(i, LAG_D + 2 * LAG, functools.partial(stage_p, 1), layers)
         at(i, lag_z, stage_z, layers)
         at(i, lag_z + 1, stage_f, layers - 1)
-        return carry
-
-    lax.fori_loop(0, layers + lag_z, step, 0)
+
+    def fill(i, carry):
+        wait_a(i)
+        work_a(i)
+        send_pair(i)
+        pl.when(i + SLOTS < layers)(lambda: b_start(i + SLOTS))
+        return carry
+
+    def steady(i, carry):
+        wait_d(i - LAG_D)
+        wait_a(i)
+        work_d(i - LAG_D)
+        work_a(i)
+        send_pair(i)
+        send_d(i - LAG_D)
+        pl.when(i + SLOTS < layers)(lambda: b_start(i + SLOTS))
+        exchange(i)
+        return carry
+
+    def drain(i, carry):
+        @pl.when(i < layers + LAG_D)
+        def _():
+            wait_d(i - LAG_D)
+            work_d(i - LAG_D)
+            send_d(i - LAG_D)
+
+        exchange(i)
+        return carry
+
+    lax.fori_loop(0, LAG_D, fill, 0)
+    for layer in range(layers):
+        for j in range(2):
+            for k in range(chunks):
+                old_pack[layer, j, k:k + 1, :] = lane_old[j, layer:layer + 1, k * LANES:(k + 1) * LANES]
+            old_pack[layer, j, chunks:, :] = jnp.ones((half - chunks, LANES), jnp.float32)
+    lax.fori_loop(LAG_D, layers, steady, 0)
+    lax.fori_loop(layers, layers + lag_z, drain, 0)
 
     for layer in range(layers):
         role = pair(layer)[1]
@@ -315,13 +349,13 @@
         vm = pltpu.VMEM
         dma = pltpu.SemaphoreType.DMA
         scratch = [
-            pltpu.SMEM((3,), f32), vm((layers, 2 * depth, tokens), jnp.bfloat16), vm((SLOTS, tokens, width), jnp.bfloat16),
+            pltpu.SMEM((3,), f32), vm((layers, 2 * depth, tokens), jnp.bfloat16), vm((layers, depth, tokens), jnp.bfloat16), vm((SLOTS, tokens, width), jnp.bfloat16),
             vm((layers, 2 * depth, width), f32), vm((layers, depth, width), f32),
             vm((2, layers, depth), f32), vm((2, layers, width), f32), vm((layers, 2, half, LANES), f32),
             vm((layers, 2 * depth, LANES), f32), vm((layers, depth, LANES), f32), vm((layers, depth, LANES), f32),
             vm((2, half, LANES), f32), vm((layers, 2, half, LANES), f32), vm((layers, 2, half, LANES), f32),
             vm((layers, 2, 2 * depth + 8, LANES), f32), vm((3, layers, side, 2 * half, LANES), f32), vm((layers, 2, 8, LANES), f32),
-            dma((7,)), dma((layers,)), dma((layers,)), dma((SLOTS,)), dma((9,)), dma((layers,)), dma((layers,)), dma((layers,)), dma((3, layers)), dma((layers,)), dma((layers,)),
+            dma((5,)), dma((layers,)), dma((layers,)), dma((layers,)), dma((layers,)), dma((SLOTS,)), dma((9,)), dma((layers,)), dma((layers,)), dma((layers,)), dma((3, layers)), dma((layers,)), dma((layers,)),
         ]
         in_vmem = pl.BlockSpec(memory_space=vm)
         anywhere = pl.BlockSpec(memory_space=pl.ANY)

time: 47.9 us -> 44 us (0.919)
  Pallas kernels: 47.1 us -> 43.2 us
    pallas_call x1, Pallas kernels: 45.4 us -> 41.6 us  [local_step(): pl.pallas_call(functools.partial(kernel, side), out_shape=(vm((2, layers,...]
where the time goes in v4:
time: 44 us; the launch traced here: 43.9 us
  Pallas kernels  43.2 us (98%)
  between operations  0.64 us (1%)
    pallas_call x1, Pallas kernels, local_step(): pl.pallas_call(functools.partial(kernel, side), out_shape=(vm((2, layers,...  41.6 us
    pallas_call x1, Pallas kernels, local_step(): pl.pallas_call(write_kernel, out_shape=(shape(layers, depth, width), shap...  1.68 us

profile of v4, /device:TPU:1, one launch (start us, length us, event | category | flops | bytes accessed | tf_op | source)
XLA Modules:
  0.0 43.9 jit_solution(15952383578175473178)
XLA Ops:
  0.6 41.6 %adafactor_step.1 = (f32[2,16,16,1408]{3,2,1,0:T(8,128)S(1)}, f32[2,16,16]{2,1,0:T(8,128)S(1)}, f32[2,16,1408]{2,1,0:T(8,128)S(1)}) custom-call(f32[3]{0:T(128)} %hyper.1, bf16[16,16,1024]{2,1,0:T(8,128)(2,1)} %bitcast.5, bf16[16,1024,1408]{2,1,0:T(8,128)(2,1)} %b_in.1, f32[16,16,1408]{2,1,0:T(8,128)} %w_in.1, f32[16,16]{1,0:T(8,128)} %side_in.1, ...), custom_call_target="tpu_custom_call" | custom-call | tf_op jit(solution)/shard_map/adafactor_step/pallas_call | solution.py:362
  42.2 1.7 %write_back.1 = (f32[16,16,1408]{2,1,0:T(8,128)}, f32[16,16]{1,0:T(8,128)}, f32[16,1408]{1,0:T(8,128)}, f32[16,16,1408]{2,1,0:T(8,128)}, f32[16,1408]{1,0:T(8,128)}, /*index=5*/f32[16,16]{1,0:T(8,128)}) custom-call(f32[2,16,16,1408]{3,2,1,0:T(8,128)S(1)} %get-tuple-element.15.w_v, f32[2,16,16]{2,1,0:T(8,128)S(1)} %get-tuple-element.16.side_v, ...), custom_call_target="tpu_custom_call" | custom-call | tf_op jit(solution)/shard_map/write_back/pallas_call | solution.py:372

commit v5 on v4

--- a/solution.py
+++ b/solution.py
@@ -13,7 +13,8 @@
 LANES = 128
 SLOTS = 6
 LAG = 7
-LAG_D = 2
+LAG_D = 3
+EARLY = 6
 VMEM_LIMIT = 48 * 1024 * 1024
 
 
@@ -92,6 +93,20 @@
     lax.fori_loop(0, layers, load_a, 0)
     for s in range(SLOTS):
         b_start(s)
+
+    def send(src, dst, recv, d, k):
+        pltpu.make_async_remote_copy(src_ref=src, dst_ref=dst, send_sem=send_sem.at[k], recv_sem=recv, device_id=d, device_id_type=MESH).start()
+
+    def arrived(ref, sem):
+        pltpu.make_async_copy(ref, ref, sem).wait()
+
+    def send_a(layer):
+        arrived(ax_v.at[layer], ax_sem.at[layer])
+        send(ax_v.at[layer], a_v.at[layer, pl.ds(depth, depth)], ar_sem.at[layer], dev(pair(layer)[2], core), 0)
+
+    pl.semaphore_wait(barrier, len(peers))
+    for layer in range(EARLY):
+        send_a(layer)
     for c in small:
         c.wait()
 
@@ -102,12 +117,6 @@
     real = half_id < chunks
     left = lax.broadcasted_iota(jnp.int32, (1, LANES), 1) < LANES // 2
 
-    def send(src, dst, recv, d, k):
-        pltpu.make_async_remote_copy(src_ref=src, dst_ref=dst, send_sem=send_sem.at[k], recv_sem=recv, device_id=d, device_id_type=MESH).start()
-
-    def arrived(ref, sem):
-        pltpu.make_async_copy(ref, ref, sem).wait()
-
     old_sum = lane_old[1, :, :LANES]
     for k in range(1, chunks):
         old_sum = old_sum + lane_old[1, :, k * LANES:(k + 1) * LANES]
@@ -121,16 +130,14 @@
         side_buf[layer, :depth, :] = jnp.where(role == 0, column[0], column[1])
         side_out_buf[layer] = jnp.where(role == 0, column[1], column[0])
         pair_buf[layer, core, 2 * depth:, :] = jnp.broadcast_to(old_sum[layer:layer + 1], (8, LANES))
-    pl.semaphore_wait(barrier, len(peers))
-
-    def send_a(layer, carry):
-        _, role, mate = pair(layer)
-        arrived(ax_v.at[layer], ax_sem.at[layer])
-        send(ax_v.at[layer], a_v.at[layer, pl.ds(depth, depth)], ar_sem.at[layer], dev(mate, core), 0)
+
+    def send_side(layer, carry):
+        mate = pair(layer)[2]
         send(side_out_buf.at[layer], side_buf.at[layer, pl.ds(depth, depth)], so_sem.at[layer], dev(mate, core), 1)
-        return carry
-
-    lax.fori_loop(0, layers, send_a, 0)
+        pl.when(layer >= EARLY)(lambda: send_a(layer))
+        return carry
+
+    lax.fori_loop(0, layers, send_side, 0)
 
     def wait_a(layer):
         slot = lax.rem(layer, SLOTS)

time: 44 us -> 43.6 us (level)
  no operation moved by 1% of the time
where the time goes in v5:
time: 43.6 us; the launch traced here: 43.5 us
  Pallas kernels  42.8 us (98%)
  between operations  0.64 us (1%)
    pallas_call x1, Pallas kernels, local_step(): pl.pallas_call(functools.partial(kernel, side), out_shape=(vm((2, layers,...  41.2 us
    pallas_call x1, Pallas kernels, local_step(): pl.pallas_call(write_kernel, out_shape=(shape(layers, depth, width), shap...  1.68 us

profile of v5, /device:TPU:1, one launch (start us, length us, event | category | flops | bytes accessed | tf_op | source)
XLA Modules:
  0.0 43.5 jit_solution(11139786249097225138)
XLA Ops:
  0.6 41.2 %adafactor_step.1 = (f32[2,16,16,1408]{3,2,1,0:T(8,128)S(1)}, f32[2,16,16]{2,1,0:T(8,128)S(1)}, f32[2,16,1408]{2,1,0:T(8,128)S(1)}) custom-call(f32[3]{0:T(128)} %hyper.1, bf16[16,16,1024]{2,1,0:T(8,128)(2,1)} %bitcast.5, bf16[16,1024,1408]{2,1,0:T(8,128)(2,1)} %b_in.1, f32[16,16,1408]{2,1,0:T(8,128)} %w_in.1, f32[16,16]{1,0:T(8,128)} %side_in.1, ...), custom_call_target="tpu_custom_call" | custom-call | tf_op jit(solution)/shard_map/adafactor_step/pallas_call | solution.py:369
  41.8 1.7 %write_back.1 = (f32[16,16,1408]{2,1,0:T(8,128)}, f32[16,16]{1,0:T(8,128)}, f32[16,1408]{1,0:T(8,128)}, f32[16,16,1408]{2,1,0:T(8,128)}, f32[16,1408]{1,0:T(8,128)}, /*index=5*/f32[16,16]{1,0:T(8,128)}) custom-call(f32[2,16,16,1408]{3,2,1,0:T(8,128)S(1)} %get-tuple-element.15.w_v, f32[2,16,16]{2,1,0:T(8,128)S(1)} %get-tuple-element.16.side_v, ...), custom_call_target="tpu_custom_call" | custom-call | tf_op jit(solution)/shard_map/write_back/pallas_call | solution.py:379

commit v6 on v5

--- a/solution.py
+++ b/solution.py
@@ -13,7 +13,7 @@
 LANES = 128
 SLOTS = 6
 LAG = 7
-LAG_D = 3
+LAG_D = 4
 EARLY = 6
 VMEM_LIMIT = 48 * 1024 * 1024
 

time: 43.6 us -> 44.6 us (1.023)
  Pallas kernels: 42.8 us -> 43.8 us
    pallas_call x1, Pallas kernels: 41.2 us -> 42.2 us  [local_step(): pl.pallas_call(functools.partial(kernel, side), out_shape=(vm((2, layers,...]
where the time goes in v6:
time: 44.6 us; the launch traced here: 44.5 us
  Pallas kernels  43.8 us (98%)
  between operations  0.64 us (1%)
    pallas_call x1, Pallas kernels, local_step(): pl.pallas_call(functools.partial(kernel, side), out_shape=(vm((2, layers,...  42.2 us
    pallas_call x1, Pallas kernels, local_step(): pl.pallas_call(write_kernel, out_shape=(shape(layers, depth, width), shap...  1.68 us

profile of v6, /device:TPU:1, one launch (start us, length us, event | category | flops | bytes accessed | tf_op | source)
XLA Modules:
  0.0 44.5 jit_solution(8090571872835818830)
XLA Ops:
  0.6 42.2 %adafactor_step.1 = (f32[2,16,16,1408]{3,2,1,0:T(8,128)S(1)}, f32[2,16,16]{2,1,0:T(8,128)S(1)}, f32[2,16,1408]{2,1,0:T(8,128)S(1)}) custom-call(f32[3]{0:T(128)} %hyper.1, bf16[16,16,1024]{2,1,0:T(8,128)(2,1)} %bitcast.5, bf16[16,1024,1408]{2,1,0:T(8,128)(2,1)} %b_in.1, f32[16,16,1408]{2,1,0:T(8,128)} %w_in.1, f32[16,16]{1,0:T(8,128)} %side_in.1, ...), custom_call_target="tpu_custom_call" | custom-call | tf_op jit(solution)/shard_map/adafactor_step/pallas_call | solution.py:369
  42.8 1.7 %write_back.1 = (f32[16,16,1408]{2,1,0:T(8,128)}, f32[16,16]{1,0:T(8,128)}, f32[16,1408]{1,0:T(8,128)}, f32[16,16,1408]{2,1,0:T(8,128)}, f32[16,1408]{1,0:T(8,128)}, /*index=5*/f32[16,16]{1,0:T(8,128)}) custom-call(f32[2,16,16,1408]{3,2,1,0:T(8,128)S(1)} %get-tuple-element.15.w_v, f32[2,16,16]{2,1,0:T(8,128)S(1)} %get-tuple-element.16.side_v, ...), custom_call_target="tpu_custom_call" | custom-call | tf_op jit(solution)/shard_map/write_back/pallas_call | solution.py:379
